TPU v7x, 256 devices: a whole 4x4x8 slice. The times are simulated.
256 devices in a mesh: section: 2 (over core), dp: 16 (over z, x_lo), tensor: 8 (over y, x_hi).
Axes of the slice: x: 4 (x_hi: 2, x_lo: 2; x = x_hi * 2 + x_lo), y: 4, z: 8, core: 2. Of those that a mesh axis runs over, the one named last changes fastest.
Arguments:
- tokens: bfloat16 [2048, 4096], P('dp', 'tensor'), may hold values from -6 to 6
- gain: bfloat16 [2, 4096], P('section', 'tensor'), may hold values from 0.099609375 to 1.8984375
- w_up: bfloat16 [2, 4096, 5120], P('section', 'dp', 'tensor'), may hold values from -0.09375 to 0.09375
- w_down: bfloat16 [2, 5120, 4096], P('section', 'tensor', 'dp'), may hold values from -0.078125 to 0.078125
- cotangent: bfloat16 [2, 2048, 4096], P('section', 'dp'), may hold values from -6 to 6
Outputs:
- states: bfloat16 [2, 2048, 4096], P('section', 'dp', 'tensor')
- grad_down: bfloat16 [2, 5120, 4096], P('section', 'tensor', 'dp')
All inputs are finite; a program needn't handle non-finite values.
Results may differ from a plain program's by a relative error of at most 0.02.
Values may be sent and summed in bfloat16 or wider, within the bound.
A program may use at most 64 MiB of HBM per device.

v0:
```python
import jax
import jax.numpy as jnp
from jax import lax
from jax.sharding import Mesh
from jax.sharding import PartitionSpec as P

MICRO = 2
MB_ROWS = 64
DP = ("dp_0", "dp_1")


EPS = 1e-06


def gathered_by_axis(array, axes, dim):
    filled = array
    for number in range(len(axes) - 1, -1, -1):
        filled = lax.all_gather(filled, axes[number], axis=dim, tiled=True)
    return filled


def in_order(pieces, dim):
    dims = list(pieces.shape[1:])
    dims[dim] *= pieces.shape[0]
    return jnp.moveaxis(pieces, 0, dim).reshape(dims)


def copy_for_each(array, axis):
    peers = lax.axis_size(axis)
    return lax.all_to_all(
        jnp.broadcast_to(array[None], (peers, *array.shape)), axis, 0, 0, tiled=True
    )


def collect(array, axis, dim):
    return in_order(copy_for_each(array, axis), dim)


def split_up(array, dim, peers):
    before, after = (array.shape[:dim], array.shape[dim + 1 :])
    return jnp.moveaxis(array.reshape(*before, peers, -1, *after), dim, 0)


def summed_on_arrival(array, axis, dim):
    pieces = split_up(array, dim, lax.axis_size(axis))
    arrived = lax.all_to_all(pieces, axis, split_axis=0, concat_axis=0, tiled=True)
    return arrived.astype(jnp.float32).sum(axis=0)


def shifted(array, axis, by):
    peers = lax.axis_size(axis)
    pairs = [(i, i + by) for i in range(peers) if 0 <= i + by < peers]
    return lax.ppermute(array, axis, pairs)


def body(tokens, gain, w_up, w_down, cotangent):
    section_id = lax.axis_index("section")
    section_count = lax.axis_size("section")
    up_whole = gathered_by_axis(w_up[0], DP, 0)
    down_whole = gathered_by_axis(w_down[0], DP, 1)
    width = up_whole.shape[0]
    hidden_width = up_whole.shape[1]
    gain_own = gain[0]
    gain_whole = lax.all_gather(gain_own, "tensor", axis=0, tiled=True)
    micro_rows = MB_ROWS
    micro_count = MICRO
    own_width = tokens.shape[1]
    tok_rows = tokens.shape[0]

    def project(normed):
        pre_act = jnp.dot(normed, up_whole, preferred_element_type=jnp.float32)
        hidden = jax.nn.gelu(pre_act, approximate=True).astype(jnp.bfloat16)
        partial_value = jnp.dot(hidden, down_whole, preferred_element_type=jnp.float32).astype(
            jnp.bfloat16
        )
        return (hidden, lax.optimization_barrier(partial_value).astype(jnp.float32))

    def skipped(normed):
        return (
            jnp.zeros((micro_rows, hidden_width), jnp.bfloat16),
            jnp.zeros((micro_rows, width), jnp.float32),
        )

    def advance(step_id, loop_state):
        incoming, states, hiddens = loop_state
        micro_id = step_id - section_id
        active = (micro_id >= 0) & (micro_id < micro_count)
        slot_pos = jnp.clip(micro_id, 0, micro_count - 1) * micro_rows
        entry_rows = lax.dynamic_slice_in_dim(tokens, slot_pos, micro_rows, 0)
        current = jnp.where(section_id == 0, entry_rows, incoming)
        current_f = current.astype(jnp.float32)
        whole_rows = collect(current, "tensor", 1)
        whole_f = whole_rows.astype(jnp.float32)
        inverse_rms = lax.rsqrt(jnp.mean(whole_f * whole_f, axis=1, keepdims=True) + EPS)
        normed = (whole_f * inverse_rms * gain_whole.astype(jnp.float32)).astype(jnp.bfloat16)
        hidden, partial_value = lax.cond(active, project, skipped, normed)
        summed = summed_on_arrival(partial_value.astype(jnp.bfloat16), "tensor", 1)
        result = (current_f + summed).astype(jnp.bfloat16)
        old_state = lax.dynamic_slice_in_dim(states, slot_pos, micro_rows, 0)
        states = lax.dynamic_update_slice_in_dim(
            states, jnp.where(active, result, old_state), slot_pos, 0
        )
        old_hidden = lax.dynamic_slice_in_dim(hiddens, slot_pos, micro_rows, 0)
        hiddens = lax.dynamic_update_slice_in_dim(
            hiddens, jnp.where(active, hidden, old_hidden), slot_pos, 0
        )
        incoming = shifted(result, "section", 1)
        return (incoming, states, hiddens)

    initial = (
        jnp.zeros((micro_rows, own_width), jnp.bfloat16),
        jnp.zeros((tok_rows, own_width), jnp.bfloat16),
        jnp.zeros((tok_rows, hidden_width), jnp.bfloat16),
    )
    final_state = lax.fori_loop(0, micro_count + section_count - 1, advance, initial)
    states = final_state[1]
    hiddens = final_state[2]
    cot_own = cotangent[0]
    dp_count = lax.axis_size(DP)
    hidden_all = lax.all_gather(hiddens, DP, axis=0, tiled=True)
    cot_mine = lax.all_to_all(cot_own, DP, split_axis=1, concat_axis=0, tiled=True)
    grad_own = jnp.zeros((hidden_width, width // dp_count), jnp.float32)
    for peer_id in range(dp_count):
        lower = peer_id * tok_rows
        partial_value = lax.dot_general(
            hidden_all[lower : lower + tok_rows],
            cot_mine[lower : lower + tok_rows],
            (((0,), (0,)), ((), ())),
            preferred_element_type=jnp.float32,
        ).astype(jnp.bfloat16)
        grad_own = grad_own + lax.optimization_barrier(partial_value).astype(jnp.float32)
    return (states[None], grad_own.astype(jnp.bfloat16)[None])


def solution(mesh):
    torus = Mesh(
        mesh.devices.reshape(mesh.shape["section"], 8, 2, mesh.shape["tensor"]),
        ("section", "dp_0", "dp_1", "tensor"),
    )
    in_specs = (
        P(DP, "tensor"),
        P("section", "tensor"),
        P("section", DP, "tensor"),
        P("section", "tensor", DP),
        P("section", DP, None),
    )
    out_specs = (P("section", DP, "tensor"), P("section", "tensor", DP))
    return jax.shard_map(body, mesh=torus, in_specs=in_specs, out_specs=out_specs, check_vma=False)
```

profile of v0, /device:TPU:2, one launch (start us, length us, event | category | flops | bytes accessed | tf_op | source)
XLA Modules:
  0.0 377.0 jit_solution(14900252217565980653)
XLA Ops:
  7.2 10.4 %all-gather.1 = bf16[1,512,640]{2,1,0:T(8,128)(2,1)} all-gather(bf16[1,256,640]{2,1,0:T(8,128)(2,1)} %param.11), channel_id=3, replica_groups=mesh['section'=2,'dp_0'=8,'dp_1'=2,'tensor'=8] {'dp_1'}, dimensions={1}, use_global_device_ids=true | all-gather | bytes 983040 | tf_op jit(solution)/shard_map/all_gather | solution.py:18
  17.7 11.1 %all-gather.3 = bf16[1,640,512]{2,1,0:T(8,128)(2,1)} all-gather(bf16[1,640,256]{2,1,0:T(8,128)(2,1)} %param.12), channel_id=5, replica_groups=mesh['section'=2,'dp_0'=8,'dp_1'=2,'tensor'=8] {'dp_1'}, dimensions={2}, use_global_device_ids=true | all-gather | bytes 983040 | tf_op jit(solution)/shard_map/all_gather | solution.py:18
  29.0 31.6 %all-gather = bf16[1,4096]{1,0:T(2,128)(2,1)S(1)} all-gather(bf16[1,512]{1,0:T(2,128)(2,1)S(1)} %copy-done.7), channel_id=2, replica_groups=mesh['section'=2,'dp_0'=8,'dp_1'=2,'tensor'=8] {'tensor'}, dimensions={1}, use_global_device_ids=true | all-gather | bytes 9216 | tf_op jit(solution)/shard_map/all_gather | solution.py:64
  60.6 25.8 %all-gather.11.cloned.1.call-done = bf16[1,4096,640]{2,1,0:T(8,128)(2,1)} async-done(((bf16[1,512,640]{2,1,0:T(8,128)(2,1)}), bf16[1,4096,640]{2,1,0:T(8,128)(2,1)}) %all-gather.11.cloned.1.call-update) | async-done | bytes 5242896 | tf_op jit(solution)/shard_map/all_gather | solution.py:18
  86.5 65.0 %all-gather.13.cloned.1.call-done = bf16[1,640,4096]{2,1,0:T(8,128)(2,1)} async-done(((bf16[1,640,512]{2,1,0:T(8,128)(2,1)}), bf16[1,640,4096]{2,1,0:T(8,128)(2,1)}) %all-gather.13.cloned.1.call-update) | async-done | bytes 5242896 | tf_op jit(solution)/shard_map/all_gather | solution.py:18
  151.6 124.7 %while.18 = (s32[]{:T(128)}, bf16[64,512]{1,0:T(8,128)(2,1)S(1)}, bf16[128,512]{1,0:T(8,128)(2,1)S(1)}, bf16[128,640]{1,0:T(8,128)(2,1)S(1)}, pred[]{:T(512)}, /...) while((s32[]{:T(128)}, bf16[64,512]{1,0:T(8,128)(2,1)S(1)}, ...), condition=%wide.region_5.6_spmd, body=%wide.region_0.5_spmd.sunk | while | flops 674254912 | bytes 67036620 | solution.py:115
  151.6 0.8 broadcast_in_dim.44
  152.5 5.8 %all-to-all-start = ((bf16[8,64,512]{2,1,0:T(8,128)(2,1)}), bf16[8,64,512]{2,1,0:T(8,128)(2,1)S(1)}, u32[]{:S(2)}, u32[]{:S(2)}) async-start(bf16[8,64,512]{2,1,0:T(8,128)(2,1)} %broadcast_in_dim.44), calls=%async_computation | async-start | bytes 1048576 | tf_op jit(solution)/shard_map/while/body/eval_jaxpr/all_to_all | solution.py:30
  158.3 11.4 %all-to-all-done = bf16[8,64,512]{2,1,0:T(8,128)(2,1)S(1)} async-done(((bf16[8,64,512]{2,1,0:T(8,128)(2,1)}), bf16[8,64,512]{2,1,0:T(8,128)(2,1)S(1)}, u32[]{:S(2)}, u32[]{:S(2)}) %all-to-all-start) | async-done | bytes 524320 | tf_op jit(solution)/shard_map/while/body/eval_jaxpr/all_to_all | solution.py:30
  170.3 2.1 copy-done
  172.4 4.5 %conditional.2 = (bf16[64,640]{1,0:T(8,128)(2,1)}, bf16[64,4096]{1,0:T(8,128)(2,1)S(1)}) conditional(s32[]{:T(128)} %convert_element_type.313, () %tuple.49, (bf16[64,4096]{1,0:T(8,128)(2,1)S(1)}, bf16[4096,640]{1,0:T(8,128)(2,1)S(1)}, bf16[640,4096]{1,0:T(8,128)(2,1)}) %tuple.63), branch_computations={%region_2.2_spmd, %region_3.3_spmd} | conditional | flops 671719424 | bytes 32669740 | solution.py:96
  172.4 1.7 fusion.7
  174.1 0.9 copy-done.1
  174.9 1.9 convolution_convert_fusion
  177.1 1.0 copy.67
  178.0 3.5 all-to-all-start.1
  181.5 10.1 %all-to-all-done.1 = bf16[8,64,512]{2,1,0:T(8,128)(2,1)S(1)} async-done(((bf16[8,64,512]{2,1,0:T(8,128)(2,1)}), bf16[8,64,512]{2,1,0:T(8,128)(2,1)S(1)}, u32[]{:S(2)}, u32[]{:S(2)}) %all-to-all-start.1) | async-done | bytes 524320 | tf_op jit(solution)/shard_map/while/body/eval_jaxpr/all_to_all | solution.py:46
  191.7 1.3 collective-permute-start
  193.0 0.9 select_dynamic-update-slice_fusion.5
  194.0 0.8 broadcast_in_dim.44
  194.9 3.5 all-to-all-start
  198.4 12.2 %all-to-all-done = bf16[8,64,512]{2,1,0:T(8,128)(2,1)S(1)} async-done(((bf16[8,64,512]{2,1,0:T(8,128)(2,1)}), bf16[8,64,512]{2,1,0:T(8,128)(2,1)S(1)}, u32[]{:S(2)}, u32[]{:S(2)}) %all-to-all-start) | async-done | bytes 524320 | tf_op jit(solution)/shard_map/while/body/eval_jaxpr/all_to_all | solution.py:30
  211.2 2.1 copy-done
  213.3 4.5 %conditional.2 = (bf16[64,640]{1,0:T(8,128)(2,1)}, bf16[64,4096]{1,0:T(8,128)(2,1)S(1)}) conditional(s32[]{:T(128)} %convert_element_type.313, () %tuple.49, (bf16[64,4096]{1,0:T(8,128)(2,1)S(1)}, bf16[4096,640]{1,0:T(8,128)(2,1)S(1)}, bf16[640,4096]{1,0:T(8,128)(2,1)}) %tuple.63), branch_computations={%region_2.2_spmd, %region_3.3_spmd} | conditional | flops 671719424 | bytes 32669740 | solution.py:96
  213.3 1.7 fusion.7
  215.0 0.9 copy-done.1
  215.8 1.9 convolution_convert_fusion
  218.0 1.0 copy.67
  218.9 3.5 all-to-all-start.1
  222.4 11.1 %all-to-all-done.1 = bf16[8,64,512]{2,1,0:T(8,128)(2,1)S(1)} async-done(((bf16[8,64,512]{2,1,0:T(8,128)(2,1)}), bf16[8,64,512]{2,1,0:T(8,128)(2,1)S(1)}, u32[]{:S(2)}, u32[]{:S(2)}) %all-to-all-start.1) | async-done | bytes 524320 | tf_op jit(solution)/shard_map/while/body/eval_jaxpr/all_to_all | solution.py:46
  233.7 1.3 collective-permute-start
  235.0 0.9 select_dynamic-update-slice_fusion.5
  236.0 0.8 broadcast_in_dim.44
  236.8 3.5 all-to-all-start
  240.3 12.2 %all-to-all-done = bf16[8,64,512]{2,1,0:T(8,128)(2,1)S(1)} async-done(((bf16[8,64,512]{2,1,0:T(8,128)(2,1)}), bf16[8,64,512]{2,1,0:T(8,128)(2,1)S(1)}, u32[]{:S(2)}, u32[]{:S(2)}) %all-to-all-start) | async-done | bytes 524320 | tf_op jit(solution)/shard_map/while/body/eval_jaxpr/all_to_all | solution.py:30
  253.2 2.1 copy-done
  255.2 0.7 conditional.2
  255.2 0.6 broadcast.38
  256.1 1.0 copy.67
  257.1 3.5 all-to-all-start.1
  260.6 11.1 %all-to-all-done.1 = bf16[8,64,512]{2,1,0:T(8,128)(2,1)S(1)} async-done(((bf16[8,64,512]{2,1,0:T(8,128)(2,1)}), bf16[8,64,512]{2,1,0:T(8,128)(2,1)S(1)}, u32[]{:S(2)}, u32[]{:S(2)}) %all-to-all-start.1) | async-done | bytes 524320 | tf_op jit(solution)/shard_map/while/body/eval_jaxpr/all_to_all | solution.py:46
  271.7 3.6 collective-permute-start
  275.5 0.8 collective-permute-done
  276.3 0.7 copy-done.2
  277.0 0.7 copy.43
  277.7 38.9 %all_to_all.38 = bf16[128,16,256]{0,2,1:T(8,128)(2,1)S(1)} all-to-all(bf16[128,16,256]{0,2,1:T(8,128)(2,1)S(1)} %bitcast.112), channel_id=1, replica_groups=mesh['section'=2,'dp_0'=8,'dp_1'=2,'tensor'=8] {'dp_0','dp_1'}, dimensions={1} | all-to-all | bytes 2097152 | tf_op jit(solution)/shard_map/all_to_all | solution.py:121
  316.5 43.1 %all-gather.9.cloned.1.call-done = bf16[2048,640]{1,0:T(8,128)(2,1)} async-done(((bf16[128,640]{1,0:T(8,128)(2,1)}), bf16[2048,640]{1,0:T(8,128)(2,1)}) %all-gather.9.cloned.1.call-update) | async-done | bytes 2621456 | tf_op jit(solution)/shard_map/all_gather | solution.py:120
  359.7 1.3 convolution_convert_fusion.1
  361.0 1.2 convolution_convert_fusion.2
  362.2 1.2 convolution_convert_fusion.3
  363.4 1.2 convolution_convert_fusion.4
  364.6 1.2 convolution_convert_fusion.5
  365.9 0.3 convolution_convert_fusion.6
  366.1 0.3 convolution_convert_fusion.7
  366.4 0.3 convolution_convert_fusion.8
  366.7 0.3 convolution_convert_fusion.9
  367.0 0.3 convolution_convert_fusion.10
  367.3 0.3 convolution_convert_fusion.11
  367.6 0.3 convolution_convert_fusion.12
  367.9 0.3 convolution_convert_fusion.13
  368.1 0.3 convolution_convert_fusion.14
  368.4 0.3 convolution_convert_fusion.16
  368.7 0.3 convolution_convert_fusion.15
  369.0 1.5 fusion.9
  (60 shorter events, 3.1 us)
Async XLA Ops:
  7.2 21.8 %copy-start.7 = (bf16[1,512]{1,0:T(2,128)(2,1)S(1)}, bf16[1,512]{1,0:T(2,128)(2,1)}, u32[]{:S(2)}) copy-start(bf16[1,512]{1,0:T(2,128)(2,1)} %param.10) | copy-start | bytes 3076
  7.2 144.4 %copy-start.6 = (bf16[128,512]{1,0:T(8,128)(2,1)S(1)}, bf16[128,512]{1,0:T(8,128)(2,1)}, u32[]{:S(2)}) copy-start(bf16[128,512]{1,0:T(8,128)(2,1)} %param.9) | copy-start | bytes 393220
  7.2 79.3 %all-gather.11.cloned.1.call-start = ((), (), s32[]{:S(2)}) async-start(), calls=%async_computation.4 | async-start | bytes 5898240 | tf_op jit(solution)/shard_map/all_gather | solution.py:18
  17.7 133.8 %all-gather.13.cloned.1.call-start = ((), (), s32[]{:S(2)}) async-start(), calls=%async_computation.5 | async-start | bytes 5898240 | tf_op jit(solution)/shard_map/all_gather | solution.py:18
  28.9 330.8 %all-gather.9.cloned.1.call-start = ((), (), s32[]{:S(2)}) async-start(), calls=%async_computation.3 | async-start | bytes 2785280 | tf_op jit(solution)/shard_map/all_gather | solution.py:120
  151.5 125.4 %copy-start.5 = (bf16[1,128,4096]{2,1,0:T(8,128)(2,1)S(1)}, bf16[1,128,4096]{2,1,0:T(8,128)(2,1)}, u32[]{:S(2)}) copy-start(bf16[1,128,4096]{2,1,0:T(8,128)(2,1)} %param.13) | copy-start | bytes 3145732
  152.5 17.2 %all-to-all-start = ((bf16[8,64,512]{2,1,0:T(8,128)(2,1)}), bf16[8,64,512]{2,1,0:T(8,128)(2,1)S(1)}, u32[]{:S(2)}, u32[]{:S(2)}) async-start(bf16[8,64,512]{2,1,0:T(8,128)(2,1)} %broadcast_in_dim.44), calls=%async_computation | async-start | bytes 1048576 | tf_op jit(solution)/shard_map/while/body/eval_jaxpr/all_to_all | solution.py:30
  169.9 2.5 copy-start
  172.4 2.5 copy-start.1
  178.0 13.6 %all-to-all-start.1 = ((bf16[8,64,512]{2,1,0:T(8,128)(2,1)}), bf16[8,64,512]{2,1,0:T(8,128)(2,1)S(1)}, u32[]{:S(2)}, u32[]{:S(2)}) async-start(bf16[8,64,512]{2,1,0:T(8,128)(2,1)} %copy.67), calls=%async_computation.1 | async-start | bytes 1048576 | tf_op jit(solution)/shard_map/while/body/eval_jaxpr/all_to_all | solution.py:46
  191.7 2.2 collective-permute-start
  194.9 15.7 %all-to-all-start = ((bf16[8,64,512]{2,1,0:T(8,128)(2,1)}), bf16[8,64,512]{2,1,0:T(8,128)(2,1)S(1)}, u32[]{:S(2)}, u32[]{:S(2)}) async-start(bf16[8,64,512]{2,1,0:T(8,128)(2,1)} %broadcast_in_dim.44), calls=%async_computation | async-start | bytes 1048576 | tf_op jit(solution)/shard_map/while/body/eval_jaxpr/all_to_all | solution.py:30
  210.8 2.5 copy-start
  213.3 2.5 copy-start.1
  218.9 14.6 %all-to-all-start.1 = ((bf16[8,64,512]{2,1,0:T(8,128)(2,1)}), bf16[8,64,512]{2,1,0:T(8,128)(2,1)S(1)}, u32[]{:S(2)}, u32[]{:S(2)}) async-start(bf16[8,64,512]{2,1,0:T(8,128)(2,1)} %copy.67), calls=%async_computation.1 | async-start | bytes 1048576 | tf_op jit(solution)/shard_map/while/body/eval_jaxpr/all_to_all | solution.py:46
  233.7 2.2 collective-permute-start
  236.8 15.7 %all-to-all-start = ((bf16[8,64,512]{2,1,0:T(8,128)(2,1)}), bf16[8,64,512]{2,1,0:T(8,128)(2,1)S(1)}, u32[]{:S(2)}, u32[]{:S(2)}) async-start(bf16[8,64,512]{2,1,0:T(8,128)(2,1)} %broadcast_in_dim.44), calls=%async_computation | async-start | bytes 1048576 | tf_op jit(solution)/shard_map/while/body/eval_jaxpr/all_to_all | solution.py:30
  252.8 2.5 copy-start
  257.1 14.6 %all-to-all-start.1 = ((bf16[8,64,512]{2,1,0:T(8,128)(2,1)}), bf16[8,64,512]{2,1,0:T(8,128)(2,1)S(1)}, u32[]{:S(2)}, u32[]{:S(2)}) async-start(bf16[8,64,512]{2,1,0:T(8,128)(2,1)} %copy.67), calls=%async_computation.1 | async-start | bytes 1048576 | tf_op jit(solution)/shard_map/while/body/eval_jaxpr/all_to_all | solution.py:46
  271.7 4.5 %collective-permute-start = (bf16[64,512]{1,0:T(8,128)(2,1)S(1)}, bf16[64,512]{1,0:T(8,128)(2,1)S(1)}, u32[]{:S(2)}, u32[]{:S(2)}) collective-permute-start(bf16[64,512]{1,0:T(8,128)(2,1)S(1)} %get-tuple-element.299), channel_id=1, source_target_pairs={{0,128},{1,129},{2,130},{3,131},{4,132},{5,133},{6,134},{7,135},{8... | collective-permute-start | bytes 196616 | tf_op jit(solution)/shard_map/while/body/eval_jaxpr/ppermute | solution.py:53
  276.3 0.7 copy-start.2
  276.3 86.0 %copy-start.4 = (bf16[128,512]{1,0:T(8,128)(2,1)}, bf16[128,512]{1,0:T(8,128)(2,1)S(1)}, u32[]{:S(2)}) copy-start(bf16[128,512]{1,0:T(8,128)(2,1)S(1)} %get-tuple-element.209) | copy-start | bytes 393220
  359.7 6.2 %copy-start.3 = (bf16[2048,640]{1,0:T(8,128)(2,1)S(1)}, bf16[2048,640]{1,0:T(8,128)(2,1)}, u32[]{:S(2)}) copy-start(bf16[2048,640]{1,0:T(8,128)(2,1)} %all-gather.9.cloned.1.call-done) | copy-start | bytes 7864324
Sparse Core Ops, SparseCore 0:
  17.8 68.6 all-gather.10
  88.3 63.1 all-gather.12
  277.1 82.5 all-gather.8
where the time goes:
time: 378 us; the launch traced here: 377 us
  waiting for transfers between devices  203 us (54%)
  blocking collectives  92.1 us (24%)
  starting transfers between devices  29.6 us (8%)
  matrix products  16.4 us (4%)
  local copies, waits for them, and re-layouts  16.2 us (4%)
  between operations  14 us (4%)
  other arithmetic  5.33 us (1%)
    all_gather x2, waiting for transfers between devices, gathered_by_axis(): filled = lax.all_gather(filled, axes[number], axis=dim, tiled=True)  90.9 us
    all_gather x1, waiting for transfers between devices, body(): hidden_all = lax.all_gather(hiddens, DP, axis=0, tiled=True)  43.1 us
    all_to_all x1, blocking collectives, body(): lax.all_to_all(cot_own, DP, split_axis=1, concat_axis=0, tiled=True)  38.9 us
    all_to_all x3, waiting for transfers between devices, copy_for_each(): lax.all_to_all(jnp.broadcast_to(array[None], (peers, *array.shape)), axis...  35.8 us
    all_to_all x3, waiting for transfers between devices, summed_on_arrival(): lax.all_to_all(pieces, axis, split_axis=0, concat_axis=0, tiled=True)  32.3 us
    all_gather x1, blocking collectives, body(): gain_whole = lax.all_gather(gain_own, 'tensor', axis=0, tiled=True)  31.6 us
    all_gather x2, blocking collectives, gathered_by_axis(): filled = lax.all_gather(filled, axes[number], axis=dim, tiled=True)  21.6 us
    all_to_all x3, starting transfers between devices, copy_for_each(): lax.all_to_all(jnp.broadcast_to(array[None], (peers, *array.shape)), axis...  12.8 us
  transfers between devices with their start and end apart: 12, of which 10 were waited for; matrix products, arithmetic and copies ran while one was open for 1% of the time, Pallas kernels for 0%

commit v1 on v0

v1 whole, which is shorter than its diff:
```python
import jax
import jax.numpy as jnp
from jax import lax
from jax.experimental import pallas as pl
from jax.experimental.pallas import tpu as pltpu
from jax.sharding import Mesh
from jax.sharding import PartitionSpec as P

NZ, NA, NY, NB = 8, 2, 4, 2
NT = NY * NB
NP = NA * NT
EPS = 1e-06
MESH = pl.DeviceIdType.MESH
F32 = jnp.float32
BF16 = jnp.bfloat16
OFFSETS = [(da, dy, db) for da in range(NA) for dy in range(NY) for db in range(NB)]
NT_DIMS = (((1,), (1,)), ((), ()))


def remote(src, dst, send, recv, **where):
    return pltpu.make_async_remote_copy(
        src_ref=src, dst_ref=dst, send_sem=send, recv_sem=recv, device_id=where, device_id_type=MESH
    )


def ring_parts(buf, z, right_send, right_recv, left_send, left_recv):
    rows = buf.shape[1] // 2

    def part(origin, half):
        return buf.at[origin, pl.ds(half * rows, rows), :]

    def right(r):
        half = r % 2
        piece = part(lax.rem(z + NZ - r // 2, NZ), half)
        return remote(piece, piece, right_send.at[r], right_recv.at[r], z=lax.rem(z + 1, NZ))

    def left(r):
        half = 1 if r == 6 else r % 2
        piece = part(lax.rem(z + r // 2, NZ), half)
        return remote(piece, piece, left_send.at[r], left_recv.at[r], z=lax.rem(z + NZ - 1, NZ))

    def from_left(r):
        piece = part(lax.rem(z + 2 * NZ - 1 - r // 2, NZ), r % 2)
        return remote(piece, piece, right_send.at[r], right_recv.at[r], z=lax.rem(z + 1, NZ))

    def from_right(r):
        half = 1 if r == 6 else r % 2
        piece = part(lax.rem(z + 1 + r // 2, NZ), half)
        return remote(piece, piece, left_send.at[r], left_recv.at[r], z=lax.rem(z + NZ - 1, NZ))

    return right, left, from_left, from_right


def ring_start(ring):
    right, left, _, _ = ring
    for r in (0, 1):
        right(r).start()
        left(r).start()


def ring_arrive(ring, r):
    right, left, from_left, from_right = ring
    from_left(r).wait_recv()
    if r + 2 <= 6:
        if r != 5:
            right(r + 2).start()
    from_right(r).wait_recv()
    if r in (0, 1, 2, 3):
        left(r + 2).start()
    if r == 5:
        left(6).start()


def ring_drain(ring):
    right, left, _, _ = ring
    for r in range(7):
        right(r).wait_send()
        left(r).wait_send()


def kernel(
    tokens, gain, up_t, down, cot, states, grad,
    up_all, down_all, x_all, h_all, h_own, c_z, c_all, gain_all, part_send, part_recv,
    x_own, result, acc_h, acc_g, g_send, g_recv,
    ex_send, ex_recv, own_sem, gain_send, gain_recv, x_send, x_recv, p_send, p_recv,
    cz_send, cz_recv, ca_send, ca_recv, next_send, next_recv, g_ssem, g_rsem,
    rs0, rr0, ls0, lr0, rs1, rr1, ls1, lr1, rs2, rr2, ls2, lr2, gate,
):
    s = lax.axis_index("section")
    z = lax.axis_index("z")
    a = lax.axis_index("a")
    y = lax.axis_index("y")
    b = lax.axis_index("b")
    t = y * NB + b
    first = s == 0
    second = s == 1
    half = up_t.shape[0] // 2
    cols = up_t.shape[1]
    rows = tokens.shape[0]
    slab = tokens.shape[1]
    sub = rows // NT
    other_a = 1 - a

    def peer(o):
        da, dy, db = OFFSETS[o]
        return {"a": lax.rem(a + da, NA), "y": lax.rem(y + dy, NY), "b": lax.rem(b + db, NB)}

    def source(o):
        da, dy, db = OFFSETS[o]
        return (
            lax.rem(a + da, NA),
            lax.rem(y + NY - dy, NY),
            lax.rem(b + db, NB),
        )

    @pl.when(first)
    def _():
        pltpu.make_async_copy(tokens, x_own, own_sem.at[4]).start()

    my_rows = pl.ds(pl.multiple_of(half * a, half), half)
    my_cols = pl.ds(pl.multiple_of(cols * a, cols), cols)
    own_up = pltpu.make_async_copy(up_t.at[my_rows, :], up_all.at[z, :, my_cols], own_sem.at[0])
    own_down = pltpu.make_async_copy(down.at[my_rows, :], down_all.at[z, :, my_cols], own_sem.at[1])
    own_gain = pltpu.make_async_copy(gain, gain_all.at[t], own_sem.at[2])
    cot_rows = pl.ds(pl.multiple_of(sub * t, sub), sub)

    def cot_cols(index):
        return pl.ds(pl.multiple_of(slab * index, slab), slab)

    own_cot = pltpu.make_async_copy(cot.at[cot_rows, cot_cols(z)], c_z.at[z], own_sem.at[3])
    own_up.start()
    own_down.start()
    own_gain.start()
    own_cot.start()

    barrier = pltpu.get_barrier_semaphore()
    for dz in range(1, NZ):
        pl.semaphore_signal(barrier, inc=1, device_id={"z": lax.rem(z + dz, NZ)}, device_id_type=MESH)
    for o in range(1, NP):
        pl.semaphore_signal(barrier, inc=1, device_id=peer(o), device_id_type=MESH)
    pl.semaphore_signal(barrier, inc=1, device_id={"section": 1 - s}, device_id_type=MESH)
    pl.semaphore_wait(barrier, NZ - 1 + NP - 1 + 1)

    their_rows = pl.ds(pl.multiple_of(half * other_a, half), half)
    ex_up = remote(up_t.at[their_rows, :], up_all.at[z, :, my_cols], ex_send.at[0], ex_recv.at[0], a=other_a)
    ex_down = remote(down.at[their_rows, :], down_all.at[z, :, my_cols], ex_send.at[1], ex_recv.at[1], a=other_a)
    ex_up.start()

    def gain_copy(o):
        return remote(gain, gain_all.at[t], gain_send.at[o], gain_recv.at[o], **peer(o))

    for o in range(1, NT):
        gain_copy(o).start()

    x_slot = x_all.at[t, pl.ds(pl.multiple_of(rows * a, rows), rows), :]
    x_mine = pltpu.make_async_copy(x_own, x_slot, own_sem.at[5])

    def x_copy(o):
        return remote(x_own, x_slot, x_send.at[o], x_recv.at[o], **peer(o))

    def x_start():
        x_mine.start()
        for o in range(1, NP):
            x_copy(o).start()

    def x_wait():
        x_mine.wait()
        for o in range(1, NP):
            sa, sy, sb = source(o)
            slot = x_all.at[sy * NB + sb, pl.ds(pl.multiple_of(rows * sa, rows), rows), :]
            remote(x_own, slot, x_send.at[o], x_recv.at[o], **peer(o)).wait_recv()
        for o in range(1, NT):
            sa, sy, sb = source(o)
            remote(gain, gain_all.at[sy * NB + sb], gain_send.at[o], gain_recv.at[o], **peer(o)).wait_recv()

    @pl.when(first)
    def _():
        pltpu.make_async_copy(tokens, x_own, own_sem.at[4]).wait()
        x_start()

    ex_down.start()

    def cz_copy(dz):
        to = lax.rem(z + dz, NZ)
        return remote(cot.at[cot_rows, cot_cols(to)], c_z.at[z], cz_send.at[dz], cz_recv.at[dz], z=to)

    def cz_start():
        for dz in range(1, NZ):
            cz_copy(dz).start()

    place = a * NT + t
    c_mine = pltpu.make_async_copy(c_z, c_all.at[place], own_sem.at[6])

    def ca_copy(o):
        return remote(c_z, c_all.at[place], ca_send.at[o], ca_recv.at[o], **peer(o))

    def ca_start():
        own_cot.wait()
        for dz in range(1, NZ):
            slot = c_z.at[lax.rem(z + NZ - dz, NZ)]
            remote(slot, slot, cz_send.at[dz], cz_recv.at[dz], z=lax.rem(z + dz, NZ)).wait_recv()
        c_mine.start()
        for o in range(1, NP):
            ca_copy(o).start()

    def ca_wait():
        c_mine.wait()
        for o in range(1, NP):
            sa, sy, sb = source(o)
            remote(c_z, c_all.at[sa * NT + sy * NB + sb], ca_send.at[o], ca_recv.at[o], **peer(o)).wait_recv()

    @pl.when(second)
    def _():
        cz_start()
        ca_start()

    own_gain.wait()
    own_up.wait()
    own_down.wait()

    up_ring = ring_parts(up_all, z, rs0, rr0, ls0, lr0)
    down_ring = ring_parts(down_all, z, rs1, rr1, ls1, lr1)
    h_ring = ring_parts(h_all, z, rs2, rr2, ls2, lr2)

    ex_up.wait_recv()

    @pl.when(second)
    def _():
        pl.semaphore_wait(gate, 1)

    ring_start(up_ring)
    for r in range(7):
        ring_arrive(up_ring, r)
    ex_down.wait_recv()
    ring_start(down_ring)

    def up_product():
        acc_h[...] = jnp.zeros_like(acc_h)

        def step(index, squares):
            block = x_all[index].astype(F32)
            squares = squares + jnp.sum(block * block, axis=1, keepdims=True)
            scaled = (block * gain_all[index]).astype(BF16)
            acc_h[...] += lax.dot_general(scaled, up_all[index], NT_DIMS, preferred_element_type=F32)
            return squares

        squares = lax.fori_loop(0, NT, step, jnp.zeros((NA * rows, 1), F32))
        inverse_rms = lax.rsqrt(squares * (1.0 / (NT * slab)) + EPS)
        hidden = jax.nn.gelu(acc_h[...] * inverse_rms, approximate=True).astype(BF16)
        h_own[...] = hidden
        h_all[z] = hidden.T

    def part_copy(index, to_a):
        to_y, to_b = index // NB, lax.rem(index, NB)
        offset = (
            lax.rem(to_a + NA - a, NA) * NT
            + lax.rem(to_y + NY - y, NY) * NB
            + lax.rem(to_b + NB - b, NB)
        )
        piece = part_send.at[index, pl.ds(to_a * rows, rows), :]
        copy = remote(
            piece, part_recv.at[offset], p_send.at[offset], p_recv.at[offset], a=to_a, y=to_y, b=to_b
        )
        return offset, copy

    def down_product(index):
        part_send[index] = lax.dot_general(
            h_own[...], down_all[index], (((1,), (0,)), ((), ())), preferred_element_type=F32
        ).astype(BF16)
        for to_a in range(NA):
            offset, copy = part_copy(index, to_a)

            @pl.when(offset != 0)
            def _():
                copy.start()

    @pl.when(first)
    def _():
        x_wait()
        up_product()
        for r in range(7):
            ring_arrive(down_ring, r)
            if r == 0:
                down_product(z)
            if r in (1, 3, 5):
                down_product(lax.rem(z + NZ - 1 - r // 2, NZ))
                down_product(lax.rem(z + 1 + r // 2, NZ))
        down_product(lax.rem(z + 4, NZ))
        pl.semaphore_signal(gate, inc=1, device_id={"section": 1 - s}, device_id_type=MESH)

    @pl.when(second)
    def _():
        for r in range(7):
            ring_arrive(down_ring, r)
        remote(result, x_own, next_send, next_recv, section=1 - s).wait_recv()
        x_start()
        x_wait()
        up_product()

        @pl.loop(0, NZ)
        def _(k):
            down_product(lax.rem(z + k, NZ))

    def finish_states():
        mine = part_send[t, pl.ds(pl.multiple_of(rows * a, rows), rows), :]
        for o in range(1, NP):
            pltpu.make_async_copy(part_recv.at[o], part_recv.at[o], p_recv.at[o]).wait()

        def add(o, total):
            return total + part_recv[o].astype(F32)

        total = lax.fori_loop(1, NP, add, x_own[...].astype(F32) + mine.astype(F32))
        result[...] = total.astype(BF16)
        states[...] = result[...]

    hand_on = remote(result, x_own, next_send, next_recv, section=1 - s)

    @pl.when(first)
    def _():
        finish_states()
        hand_on.start()
        cz_start()
        ring_start(h_ring)
        ca_start()
        for r in range(7):
            ring_arrive(h_ring, r)

    @pl.when(second)
    def _():
        ring_start(h_ring)
        for r in range(7):
            ring_arrive(h_ring, r)
        finish_states()

    ca_wait()
    acc_g[...] = jnp.zeros_like(acc_g)

    @pl.loop(0, NZ)
    def _(index):
        block = c_all[:, pl.ds(index, 1)].reshape(NP * sub, slab)
        acc_g[...] += jnp.dot(h_all[index], block, preferred_element_type=F32)

    g_send[...] = acc_g[...].astype(BF16)
    their_cols = pl.ds(pl.multiple_of(cols * other_a, cols), cols)
    swap = remote(g_send.at[:, their_cols], g_recv, g_ssem, g_rsem, a=other_a)
    swap.start()
    grad[my_rows, :] = g_send[:, my_cols]
    swap.wait_recv()
    grad[their_rows, :] = g_recv[...]

    swap.wait_send()
    ex_up.wait_send()
    ex_down.wait_send()
    for o in range(1, NT):
        gain_copy(o).wait_send()
    for o in range(1, NP):
        x_copy(o).wait_send()
        ca_copy(o).wait_send()
        pltpu.make_async_copy(part_recv.at[o], part_recv.at[o], p_send.at[o]).wait()
    for dz in range(1, NZ):
        cz_copy(dz).wait_send()

    @pl.when(first)
    def _():
        hand_on.wait_send()

    ring_drain(up_ring)
    ring_drain(down_ring)
    ring_drain(h_ring)


def body(tokens, gain, w_up, w_down, cotangent):
    rows, slab = tokens.shape
    cols, hidden = w_up.shape[1:]
    half = hidden // 2
    dma = pltpu.SemaphoreType.DMA
    vmem = pl.BlockSpec(memory_space=pltpu.VMEM)
    states, grad = pl.pallas_call(
        kernel,
        out_shape=(
            jax.ShapeDtypeStruct((rows, slab), BF16),
            jax.ShapeDtypeStruct((hidden, cols), BF16),
        ),
        in_specs=[vmem] * 5,
        out_specs=(vmem, vmem),
        scratch_shapes=[
            pltpu.VMEM((NZ, half, NA * cols), BF16),
            pltpu.VMEM((NZ, half, NA * cols), BF16),
            pltpu.VMEM((NT, NA * rows, slab), BF16),
            pltpu.VMEM((NZ, half, NA * rows), BF16),
            pltpu.VMEM((NA * rows, half), BF16),
            pltpu.VMEM((NZ, rows // NT, slab), BF16),
            pltpu.VMEM((NP, NZ, rows // NT, slab), BF16),
            pltpu.VMEM((NT, 1, slab), F32),
            pltpu.VMEM((NZ, NA * rows, slab), BF16),
            pltpu.VMEM((NP, rows, slab), BF16),
            pltpu.VMEM((rows, slab), BF16),
            pltpu.VMEM((rows, slab), BF16),
            pltpu.VMEM((NA * rows, half), F32),
            pltpu.VMEM((half, NA * cols), F32),
            pltpu.VMEM((half, NA * cols), BF16),
            pltpu.VMEM((half, cols), BF16),
            dma((2,)), dma((2,)), dma((7,)), dma((NT,)), dma((NT,)), dma((NP,)), dma((NP,)), dma((NP,)), dma((NP,)),
            dma((NZ,)), dma((NZ,)), dma((NP,)), dma((NP,)), dma, dma, dma, dma,
        ]
        + [dma((7,))] * 12
        + [pltpu.SemaphoreType.REGULAR],
        compiler_params=pltpu.CompilerParams(
            collective_id=0, has_side_effects=True, vmem_limit_bytes=48 * 1024 * 1024
        ),
    )(tokens, gain.astype(F32), w_up[0].T, w_down[0], cotangent[0])
    return states[None], grad[None]


def solution(mesh):
    torus = Mesh(
        mesh.devices.reshape(mesh.shape["section"], NZ, NA, NY, NB), ("section", "z", "a", "y", "b")
    )
    dp, tensor = ("z", "a"), ("y", "b")
    in_specs = (
        P(dp, tensor),
        P("section", tensor),
        P("section", dp, tensor),
        P("section", tensor, dp),
        P("section", dp, None),
    )
    out_specs = (P("section", dp, tensor), P("section", tensor, dp))
    return jax.shard_map(body, mesh=torus, in_specs=in_specs, out_specs=out_specs, check_vma=False)
```

time: 378 us -> 160 us (0.42)
  the two profiles are of different devices: /device:TPU:2 before, /device:TPU:35 now
where the time goes in v1:
time: 160 us
  Pallas kernels  154 us (96%)
  local copies, waits for them, and re-layouts  4.48 us (3%)
    pallas_call x1, Pallas kernels, body(): pl.pallas_call(kernel, out_shape=(jax.ShapeDtypeStruct((rows, slab), BF16...  154 us
    unnamed x11, local copies, waits for them, and re-layouts  4.48 us

profile of v1, /device:TPU:35, one launch (start us, length us, event | category | flops | bytes accessed | tf_op | source)
XLA Modules:
  0.0 159.5 jit_solution(2425120394977312182)
XLA Ops:
  0.6 0.0 copy-start.3
  0.6 0.7 copy-done.3
  1.3 0.0 copy-start.1
  1.3 0.0 copy-start.2
  1.3 1.2 copy.7
  2.5 0.0 copy-done.1
  2.5 0.0 copy-done.2
  2.5 0.0 copy-start
  2.6 1.2 copy-done
  3.8 154.4 %shard_map.68 = (bf16[128,512]{1,0:T(8,128)(2,1)S(1)}, bf16[640,256]{1,0:T(8,128)(2,1)S(1)}) custom-call(bf16[128,512]{1,0:T(8,128)(2,1)S(1)} %copy-done.2, f32[1,512]{1,0:T(1,128)S(1)} %convert_element_type.3.gain, bf16[640,256]{1,0:T(8,128)(2,1)S(1)} %bitcast.7, bf16[640,256]{1,0:T(8,128)(2,1)S(1)} %bitcast.10, bf16[128,4096]{1,0:T(8,128)(2,1)S(1)} %bitcast.8), custom_call_target="tpu_custom_call" | custom-call | tf_op jit(solution)/shard_map/pallas_call | solution.py:378
  158.1 0.7 copy.10
  158.8 0.7 copy.11
  (1 shorter events, 0.0 us)
Async XLA Ops:
  0.6 0.7 copy-start.3
  1.3 1.2 copy-start.1
  1.3 1.2 copy-start.2
  2.5 1.2 copy-start

commit v2 on v1

v2 whole, which is shorter than its diff:
```python
import jax
import jax.numpy as jnp
from jax import lax
from jax.experimental import pallas as pl
from jax.experimental.pallas import tpu as pltpu
from jax.sharding import Mesh
from jax.sharding import PartitionSpec as P

NZ, NA, NY, NB = 8, 2, 4, 2
NT = NY * NB
NP = NA * NT
STEPS = NZ // 2 + 1
EPS = 1e-06
MESH = pl.DeviceIdType.MESH
F32 = jnp.float32
BF16 = jnp.bfloat16
OFFSETS = [(da, dy, db) for da in range(NA) for dy in range(NY) for db in range(NB)]
X_OFFSETS = [(1, 0, 0), (0, 0, 1), (1, 0, 1)]
Y_OFFSETS = [(0, dy, 0) for dy in range(1, NY)]
ROW_ROW = (((1,), (1,)), ((), ()))
COL_COL = (((0,), (0,)), ((), ()))


def remote(src, dst, send, recv, **where):
    return pltpu.make_async_remote_copy(
        src_ref=src, dst_ref=dst, send_sem=send, recv_sem=recv, device_id=where, device_id_type=MESH
    )


class Ring:
    def __init__(self, z, cut, piece, sems):
        self.z, self.cut, self.piece = z, cut, piece
        self.right_send, self.right_recv, self.left_send, self.left_recv = sems
        self.count = 7 * cut // 2

    def _copy(self, origin, q, to_right, r):
        piece = self.piece(lax.rem(origin, NZ), q)
        if to_right:
            return remote(piece, piece, self.right_send.at[r], self.right_recv.at[r], z=lax.rem(self.z + 1, NZ))
        return remote(piece, piece, self.left_send.at[r], self.left_recv.at[r], z=lax.rem(self.z + NZ - 1, NZ))

    def _left_q(self, r):
        return r % self.cut + (self.cut // 2 if r // self.cut == 3 else 0)

    def right(self, r):
        return self._copy(self.z + NZ - r // self.cut, r % self.cut, True, r)

    def left(self, r):
        return self._copy(self.z + r // self.cut, self._left_q(r), False, r)

    def start(self, r):
        self.right(r).start()
        self.left(r).start()

    def arrive(self, r):
        self._copy(self.z + 2 * NZ - 1 - r // self.cut, r % self.cut, True, r).wait_recv()
        if r + self.cut < self.count:
            self.right(r + self.cut).start()
        self._copy(self.z + 1 + r // self.cut, self._left_q(r), False, r).wait_recv()
        if r < 2 * self.cut:
            self.left(r + self.cut).start()
        elif 5 * self.cut // 2 <= r < 3 * self.cut:
            self.left(r + self.cut // 2).start()

    def arrive_step(self, k):
        for r in range(self.cut * (k - 1), min(self.cut * k, self.count)):
            self.arrive(r)

    def drain(self):
        for r in range(self.count):
            self.right(r).wait_send()
            self.left(r).wait_send()


class Plane:
    def __init__(self, me, own, slot, sems):
        self.me, self.own, self.slot = me, own, slot
        self.send1, self.recv1, self.send2, self.recv2 = sems

    def _at(self, *offsets):
        a, y, b = self.me
        for da, dy, db in offsets:
            a, y, b = lax.rem(a + NA - da, NA), lax.rem(y + NY - dy, NY), lax.rem(b + NB - db, NB)
        return a, y, b

    def _peer(self, offset):
        a, y, b = self.me
        da, dy, db = offset
        return {"a": lax.rem(a + da, NA), "y": lax.rem(y + dy, NY), "b": lax.rem(b + db, NB)}

    def _first(self, half, i, origin):
        offset = (X_OFFSETS, Y_OFFSETS)[half][i]
        n = 3 * half + i
        return remote(self.own(half), self.slot(origin, half), self.send1.at[n], self.recv1.at[n], **self._peer(offset))

    def _second(self, half, source, i, piece, origin):
        offset = (Y_OFFSETS, X_OFFSETS)[half][i]
        n = 12 * half + 3 * source + i
        return remote(piece, self.slot(origin, half), self.send2.at[n], self.recv2.at[n], **self._peer(offset))

    def start(self):
        for half in (0, 1):
            for i in range(3):
                self._first(half, i, self.me).start()
        for half in (0, 1):
            for i in range(3):
                self._second(half, 0, i, self.own(half), self.me).start()

    def relay(self):
        for i in range(3):
            for half in (0, 1):
                origin = self._at((X_OFFSETS, Y_OFFSETS)[half][i])
                self._first(half, i, origin).wait_recv()
                piece = self.slot(origin, half)
                for n in range(3):
                    self._second(half, i + 1, n, piece, origin).start()

    def wait(self):
        for half in (0, 1):
            for source in range(4):
                for i in range(3):
                    hops = [(Y_OFFSETS, X_OFFSETS)[half][i]]
                    if source:
                        hops.append((X_OFFSETS, Y_OFFSETS)[half][source - 1])
                    origin = self._at(*hops)
                    self._second(half, source, i, self.own(half), origin).wait_recv()

    def drain(self):
        for half in (0, 1):
            for i in range(3):
                self._first(half, i, self.me).wait_send()
            for source in range(4):
                for i in range(3):
                    self._second(half, source, i, self.own(half), self.me).wait_send()


def kernel(
    tokens, gain, up_t, down, cot, states, grad,
    up_all, down_all, x_all, x1_all, h_all, h_own, c_z, c_all, gain_all, part_send, part_recv, sums, final,
    acc_h, acc_g, g_send, g_recv,
    ex_send, ex_recv, own_sem, gain_send, gain_recv, rs_send, rs_recv, ag_send, ag_recv, f_send, f_recv,
    cz_send, cz_recv, back_send, back_recv, g_ssem, g_rsem,
    u0, u1, u2, u3, d0, d1, d2, d3, h0, h1, h2, h3, x0, x1, x2, x3, c0, c1, c2, c3, gate,
):
    s = lax.axis_index("section")
    z = lax.axis_index("z")
    a = lax.axis_index("a")
    y = lax.axis_index("y")
    b = lax.axis_index("b")
    t = y * NB + b
    place = a * NT + t
    me = (a, y, b)
    first = s == 0
    second = s == 1
    half = up_t.shape[0] // 2
    cols = up_t.shape[1]
    rows, slab = tokens.shape
    sub = rows // NT
    other_a = 1 - a

    def peer(o):
        da, dy, db = OFFSETS[o]
        return {"a": lax.rem(a + da, NA), "y": lax.rem(y + dy, NY), "b": lax.rem(b + db, NB)}

    def source(o):
        da, dy, db = OFFSETS[o]
        return lax.rem(a + NA - da, NA), lax.rem(y + NY - dy, NY), lax.rem(b + NB - db, NB)

    my_rows = pl.ds(pl.multiple_of(half * a, half), half)
    their_rows = pl.ds(pl.multiple_of(half * other_a, half), half)
    my_cols = pl.ds(pl.multiple_of(cols * a, cols), cols)
    their_cols = pl.ds(pl.multiple_of(cols * other_a, cols), cols)
    cot_rows = pl.ds(pl.multiple_of(sub * t, sub), sub)

    def cot_cols(index):
        return pl.ds(pl.multiple_of(slab * index, slab), slab)

    def c_slot(index):
        return c_z.at[index // 4, lax.rem(index, 4)]

    own_up = pltpu.make_async_copy(up_t.at[my_rows, :], up_all.at[z, a], own_sem.at[0])
    own_down = pltpu.make_async_copy(down.at[my_rows, :], down_all.at[z, a], own_sem.at[1])
    own_gain = pltpu.make_async_copy(gain, gain_all.at[t], own_sem.at[2])
    own_cot = pltpu.make_async_copy(cot.at[cot_rows, cot_cols(z)], c_slot(z), own_sem.at[3])
    own_x = [
        pltpu.make_async_copy(tokens.at[pl.ds(rows // 2 * i, rows // 2), :], x_all.at[a, t, i], own_sem.at[4 + i])
        for i in (0, 1)
    ]
    own_c = pltpu.make_async_copy(c_z, c_all.at[place], own_sem.at[6])
    own_up.start()
    own_down.start()
    own_gain.start()
    own_cot.start()

    @pl.when(first)
    def _():
        own_x[0].start()
        own_x[1].start()

    barrier = pltpu.get_barrier_semaphore()
    for dz in range(1, NZ):
        pl.semaphore_signal(barrier, inc=1, device_id={"z": lax.rem(z + dz, NZ)}, device_id_type=MESH)
    for o in range(1, NP):
        pl.semaphore_signal(barrier, inc=1, device_id=peer(o), device_id_type=MESH)
    for o in range(NP):
        pl.semaphore_signal(barrier, inc=1, device_id=dict(peer(o), section=1 - s), device_id_type=MESH)
    own_up.wait()
    pl.semaphore_wait(barrier, NZ - 1 + NP - 1 + NP)

    ex_up = remote(up_t.at[their_rows, :], up_all.at[z, a], ex_send.at[0], ex_recv.at[0], a=other_a)
    ex_down = remote(down.at[their_rows, :], down_all.at[z, a], ex_send.at[1], ex_recv.at[1], a=other_a)
    from_up = remote(up_t.at[their_rows, :], up_all.at[z, other_a], ex_send.at[0], ex_recv.at[0], a=other_a)
    from_down = remote(down.at[their_rows, :], down_all.at[z, other_a], ex_send.at[1], ex_recv.at[1], a=other_a)
    ex_up.start()

    quarter_rows = half // 2

    def quarter(buffer):
        def piece(origin, q):
            which = a if q < 2 else other_a
            return buffer.at[origin, which, pl.ds(q % 2 * quarter_rows, quarter_rows), :]

        return piece

    up_ring = Ring(z, 4, quarter(up_all), (u0, u1, u2, u3))
    down_ring = Ring(z, 4, quarter(down_all), (d0, d1, d2, d3))
    h_ring = Ring(z, 2, lambda origin, q: h_all.at[origin, pl.ds(q * quarter_rows, quarter_rows), :], (h0, h1, h2, h3))
    x_plane = Plane(
        me,
        lambda i: tokens.at[pl.ds(rows // 2 * i, rows // 2), :],
        lambda at, i: x_all.at[at[0], at[1] * NB + at[2], i],
        (x0, x1, x2, x3),
    )
    c_plane = Plane(
        me, lambda i: c_z.at[i], lambda at, i: c_all.at[at[0] * NT + at[1] * NB + at[2], i], (c0, c1, c2, c3)
    )

    def gain_copy(o):
        return remote(gain, gain_all.at[t], gain_send.at[o], gain_recv.at[o], **peer(o))

    def cz_copy(dz):
        to = lax.rem(z + dz, NZ)
        return remote(cot.at[cot_rows, cot_cols(to)], c_slot(z), cz_send.at[dz], cz_recv.at[dz], z=to)

    def cz_start():
        for dz in range(1, NZ):
            cz_copy(dz).start()

    def cz_wait():
        own_cot.wait()
        for dz in range(1, NZ):
            slot = c_slot(lax.rem(z + NZ - dz, NZ))
            remote(slot, slot, cz_send.at[dz], cz_recv.at[dz], z=lax.rem(z + dz, NZ)).wait_recv()

    def width(k):
        return 2 if 0 < k < NZ // 2 else 1

    def slot_of(k, j):
        return lax.rem(z + (k if j else NZ - k), NZ)

    def view(buffer, k, *index):
        return buffer.at[(k, *index)] if width(k) == 2 else buffer.at[(k, *index, 0)]

    def rs_copy(k, o):
        to = peer(o)
        there = to["a"] * NT + to["y"] * NB + to["b"]
        n = k * NP + o
        return remote(view(part_send, k, there), view(part_recv, k, o), rs_send.at[n], rs_recv.at[n], **to)

    def rs_start(k):
        for o in range(1, NP):
            rs_copy(k, o).start()

    def rs_sum(k, extra):
        for o in range(1, NP):
            rs_copy(k, o).wait_recv()
        for j in range(width(k)):
            total = part_send[k, place, j].astype(F32)
            if extra is not None:
                total = total + extra(slot_of(k, j))
            for o in range(1, NP):
                total = total + part_recv[k, o, j].astype(F32)
            sums[k, j] = total.astype(BF16)

    def ag_copy(k, o):
        n = k * NP + o
        return remote(view(sums, k), view(x1_all, k, place), ag_send.at[n], ag_recv.at[n], section=1, **peer(o))

    def ag_start(k):
        for o in range(NP):
            ag_copy(k, o).start()

    def ag_wait(k):
        for o in range(NP):
            sa, sy, sb = source(o)
            n = k * NP + o
            slot = view(x1_all, k, sa * NT + sy * NB + sb)
            remote(view(sums, k), slot, ag_send.at[n], ag_recv.at[n], section=0, **peer(o)).wait_recv()

    def store_part(k, j, which, product):
        part_send[k, :, j, :, pl.ds(which * cols, cols)] = product.astype(BF16).reshape(NP, sub, cols)

    def down_first(k, j):
        for which in range(NA):
            weights = down_all[slot_of(k, j), which]
            store_part(k, j, which, jnp.dot(h_own[...], weights, preferred_element_type=F32))

    def down_second(k, j):
        for which in range(NA):
            hidden = h_all[slot_of(k, j)]
            store_part(k, j, which, lax.dot_general(hidden, down_all[z, which], COL_COL, preferred_element_type=F32))

    def up_step(block, index, squares):
        block = block.reshape(NA * rows, slab).astype(F32)
        scaled = (block * gain_all[index]).astype(BF16)
        for which in range(NA):
            acc_h[...] += lax.dot_general(
                scaled[:, which * cols : (which + 1) * cols], up_all[index, which], ROW_ROW, preferred_element_type=F32
            )
        return squares + jnp.sum(block * block, axis=1, keepdims=True)

    def finish_hidden(squares):
        inverse_rms = lax.rsqrt(squares * (1.0 / (NT * slab)) + EPS)
        hidden = jax.nn.gelu(acc_h[...] * inverse_rms, approximate=True).astype(BF16)
        h_own[...] = hidden
        h_all[z] = hidden.T

    no_squares = jnp.zeros((NA * rows, 1), F32)

    def gain_wait():
        own_gain.wait()
        for o in range(1, NT):
            _, sy, sb = source(o)
            remote(gain, gain_all.at[sy * NB + sb], gain_send.at[o], gain_recv.at[o], **peer(o)).wait_recv()

    ahead = lax.rem(t - z + NZ, NZ)
    own_k = jnp.minimum(ahead, NZ - ahead)
    own_j = 1 - jnp.minimum(lax.rem(ahead + NZ - 1, NZ) // 3, 1)
    own_states = x1_all.at[own_k, pl.ds(pl.multiple_of(NT * a, NT), NT), own_j]
    back = remote(own_states, final, back_send, back_recv, section=1 - s)

    def final_copy(k, j):
        n = 2 * k + j
        return remote(
            sums.at[k, j], final.at[t], f_send.at[n], f_recv.at[t], z=slot_of(k, j), y=z // NB, b=lax.rem(z, NB)
        )

    final_local = pltpu.make_async_copy(sums.at[0, 0], final.at[t], f_recv.at[t])

    def gradient():
        acc_g[...] = jnp.zeros_like(acc_g)

        @pl.loop(0, NZ)
        def _(index):
            block = c_all[:, index // 4, lax.rem(index, 4)].reshape(NP * sub, slab)
            acc_g[...] += jnp.dot(h_all[index], block, preferred_element_type=F32)

        g_send[...] = acc_g[...].astype(BF16)

    swap = remote(g_send.at[:, their_cols], g_recv, g_ssem, g_rsem, a=other_a)

    @pl.when(first)
    def _():
        x_plane.start()
        for r in (0, 1):
            up_ring.start(r)
        for o in range(1, NT):
            gain_copy(o).start()
        from_up.wait_recv()
        for r in (2, 3):
            up_ring.start(r)
        ex_down.start()
        up_ring.arrive(0)
        up_ring.arrive(1)
        x_plane.relay()
        for r in range(2, up_ring.count):
            up_ring.arrive(r)
        own_down.wait()
        from_down.wait_recv()
        for r in range(4):
            down_ring.start(r)
        own_x[0].wait()
        own_x[1].wait()
        x_plane.wait()
        gain_wait()
        acc_h[...] = jnp.zeros_like(acc_h)
        finish_hidden(lax.fori_loop(0, NT, lambda i, squares: up_step(x_all[:, i], i, squares), no_squares))

        def residual(index):
            return x_all[a, index, t // 4, pl.ds(pl.multiple_of(lax.rem(t, 4) * sub, sub), sub), :].astype(F32)

        for k in range(STEPS):
            if k:
                down_ring.arrive_step(k)
            for j in range(width(k)):
                down_first(k, j)
            rs_start(k)
            if k == STEPS - 1:
                pl.semaphore_signal(gate, inc=1, device_id={"section": 1 - s}, device_id_type=MESH)
            if k >= 2:
                rs_sum(k - 2, residual)
                ag_start(k - 2)
        for k in (STEPS - 2, STEPS - 1):
            rs_sum(k, residual)
            ag_start(k)
        cz_start()
        h_ring.start(0)
        h_ring.start(1)
        cz_wait()
        own_c.start()
        c_plane.start()
        h_ring.arrive(0)
        h_ring.arrive(1)
        c_plane.relay()
        for r in range(2, h_ring.count):
            h_ring.arrive(r)
        own_c.wait()
        c_plane.wait()
        gradient()
        swap.start()
        back.wait_recv()
        states[...] = final[...].reshape(rows, slab)

    @pl.when(second)
    def _():
        cz_start()
        for o in range(1, NT):
            gain_copy(o).start()
        ex_down.start()
        cz_wait()
        own_c.start()
        c_plane.start()
        c_plane.relay()
        from_up.wait_recv()
        own_down.wait()
        from_down.wait_recv()
        gain_wait()
        pl.semaphore_wait(gate, 1)
        for r in range(4):
            up_ring.start(r)
        for r in range(up_ring.count):
            up_ring.arrive(r)
        acc_h[...] = jnp.zeros_like(acc_h)
        squares = no_squares
        for k in range(STEPS):
            ag_wait(k)
            for j in range(width(k)):
                squares = up_step(x1_all[k, :, j], slot_of(k, j), squares)
        finish_hidden(squares)
        back.start()
        h_ring.start(0)
        h_ring.start(1)
        for k in range(STEPS):
            if k:
                h_ring.arrive_step(k)
            for j in range(width(k)):
                down_second(k, j)
            rs_start(k)

        own_c.wait()
        c_plane.wait()
        gradient()
        swap.start()
        at_home = (z == t)
        for k in range(STEPS):
            rs_sum(k, None)
            for j in range(width(k)):
                if k:
                    final_copy(k, j).start()
                else:
                    @pl.when(at_home)
                    def _():
                        final_local.start()

                    @pl.when(jnp.logical_not(at_home))
                    def _():
                        final_copy(0, 0).start()
        for index in range(NT):
            pltpu.make_async_copy(final.at[index], final.at[index], f_recv.at[index]).wait()
        own_rows = x1_all[own_k, pl.ds(pl.multiple_of(NT * a, NT), NT), own_j].astype(F32)
        states[...] = (own_rows + final[...].astype(F32)).astype(BF16).reshape(rows, slab)

    grad[my_rows, :] = g_send[:, my_cols]
    swap.wait_recv()
    grad[their_rows, :] = g_recv[...]

    swap.wait_send()
    ex_up.wait_send()
    ex_down.wait_send()
    for o in range(1, NT):
        gain_copy(o).wait_send()
    for dz in range(1, NZ):
        cz_copy(dz).wait_send()
    for k in range(STEPS):
        for o in range(1, NP):
            rs_copy(k, o).wait_send()
    c_plane.drain()
    up_ring.drain()
    h_ring.drain()

    @pl.when(first)
    def _():
        x_plane.drain()
        down_ring.drain()
        for k in range(STEPS):
            for o in range(NP):
                ag_copy(k, o).wait_send()

    @pl.when(second)
    def _():
        back.wait_send()
        for k in range(STEPS):
            for j in range(width(k)):
                if k:
                    final_copy(k, j).wait_send()

        @pl.when(z != t)
        def _():
            final_copy(0, 0).wait_send()


def body(tokens, gain, w_up, w_down, cotangent):
    rows, slab = tokens.shape
    cols, hidden = w_up.shape[1:]
    half = hidden // 2
    sub = rows // NT
    dma = pltpu.SemaphoreType.DMA
    vmem = pl.BlockSpec(memory_space=pltpu.VMEM)
    states, grad = pl.pallas_call(
        kernel,
        out_shape=(
            jax.ShapeDtypeStruct((rows, slab), BF16),
            jax.ShapeDtypeStruct((hidden, cols), BF16),
        ),
        in_specs=[vmem] * 5,
        out_specs=(vmem, vmem),
        scratch_shapes=[
            pltpu.VMEM((NZ, NA, half, cols), BF16),
            pltpu.VMEM((NZ, NA, half, cols), BF16),
            pltpu.VMEM((NA, NT, 2, rows // 2, slab), BF16),
            pltpu.VMEM((STEPS, NP, 2, sub, slab), BF16),
            pltpu.VMEM((NZ, half, NA * rows), BF16),
            pltpu.VMEM((NA * rows, half), BF16),
            pltpu.VMEM((2, NZ // 2, sub, slab), BF16),
            pltpu.VMEM((NP, 2, NZ // 2, sub, slab), BF16),
            pltpu.VMEM((NT, 1, slab), F32),
            pltpu.VMEM((STEPS, NP, 2, sub, slab), BF16),
            pltpu.VMEM((STEPS, NP, 2, sub, slab), BF16),
            pltpu.VMEM((STEPS, 2, sub, slab), BF16),
            pltpu.VMEM((NT, sub, slab), BF16),
            pltpu.VMEM((NA * rows, half), F32),
            pltpu.VMEM((half, NA * cols), F32),
            pltpu.VMEM((half, NA * cols), BF16),
            pltpu.VMEM((half, cols), BF16),
            dma((2,)), dma((2,)), dma((7,)), dma((NT,)), dma((NT,)),
            dma((STEPS * NP,)), dma((STEPS * NP,)), dma((STEPS * NP,)), dma((STEPS * NP,)),
            dma((2 * STEPS,)), dma((NT,)), dma((NZ,)), dma((NZ,)), dma, dma, dma, dma,
        ]
        + [dma((14,))] * 8
        + [dma((7,))] * 4
        + [dma((6,)), dma((6,)), dma((24,)), dma((24,))] * 2
        + [pltpu.SemaphoreType.REGULAR],
        compiler_params=pltpu.CompilerParams(
            collective_id=0, has_side_effects=True, vmem_limit_bytes=48 * 1024 * 1024
        ),
    )(tokens, gain.astype(F32), w_up[0].T, w_down[0], cotangent[0])
    return states[None], grad[None]


def solution(mesh):
    torus = Mesh(
        mesh.devices.reshape(mesh.shape["section"], NZ, NA, NY, NB), ("section", "z", "a", "y", "b")
    )
    dp, tensor = ("z", "a"), ("y", "b")
    in_specs = (
        P(dp, tensor),
        P("section", tensor),
        P("section", dp, tensor),
        P("section", tensor, dp),
        P("section", dp, None),
    )
    out_specs = (P("section", dp, tensor), P("section", tensor, dp))
    return jax.shard_map(body, mesh=torus, in_specs=in_specs, out_specs=out_specs, check_vma=False)
```

time: 160 us -> 111 us (0.69)
  the two profiles are of different devices: /device:TPU:35 before, /device:TPU:17 now
where the time goes in v2:
time: 111 us
  Pallas kernels  106 us (95%)
  local copies, waits for them, and re-layouts  4.48 us (4%)
    pallas_call x1, Pallas kernels, body(): pl.pallas_call(kernel, out_shape=(jax.ShapeDtypeStruct((rows, slab), BF16...  106 us
    unnamed x11, local copies, waits for them, and re-layouts  4.48 us

profile of v2, /device:TPU:17, one launch (start us, length us, event | category | flops | bytes accessed | tf_op | source)
XLA Modules:
  0.0 111.1 jit_solution(7186655032529644643)
XLA Ops:
  0.6 0.0 copy-start.3
  0.6 0.7 copy-done.3
  1.3 0.0 copy-start.1
  1.3 0.0 copy-start.2
  1.3 1.2 %copy.7 = bf16[1,256,640]{1,2,0:T(8,128)(2,1)S(1)} copy(bf16[1,256,640]{2,1,0:T(8,128)(2,1)} %param.7) | data formatting | bytes 655360 | tf_op args[2]
  2.5 0.0 copy-done.1
  2.5 0.0 copy-done.2
  2.5 0.0 copy-start
  2.6 1.2 %copy-done = bf16[1,128,4096]{2,1,0:T(8,128)(2,1)S(1)} copy-done((bf16[1,128,4096]{2,1,0:T(8,128)(2,1)S(1)}, bf16[1,128,4096]{2,1,0:T(8,128)(2,1)}, u32[]{:S(2)}) %copy-start) | copy-done | bytes 1048600
  3.8 105.9 %shard_map.68 = (bf16[128,512]{1,0:T(8,128)(2,1)S(1)}, bf16[640,256]{1,0:T(8,128)(2,1)S(1)}) custom-call(bf16[128,512]{1,0:T(8,128)(2,1)S(1)} %copy-done.2, f32[1,512]{1,0:T(1,128)S(1)} %convert_element_type.3.gain, bf16[640,256]{1,0:T(8,128)(2,1)S(1)} %bitcast.7, bf16[640,256]{1,0:T(8,128)(2,1)S(1)} %bitcast.10, bf16[128,4096]{1,0:T(8,128)(2,1)S(1)} %bitcast.8), custom_call_target="tpu_custom_call" | custom-call | tf_op jit(solution)/shard_map/pallas_call | solution.py:529
  109.7 0.7 copy.10
  110.4 0.7 copy.11
  (1 shorter events, 0.0 us)
Async XLA Ops:
  0.6 0.7 copy-start.3
  1.3 1.2 %copy-start.1 = (bf16[1,640,256]{2,1,0:T(8,128)(2,1)S(1)}, bf16[1,640,256]{2,1,0:T(8,128)(2,1)}, u32[]{:S(2)}) copy-start(bf16[1,640,256]{2,1,0:T(8,128)(2,1)} %param.8) | copy-start | bytes 983044
  1.3 1.2 %copy-start.2 = (bf16[128,512]{1,0:T(8,128)(2,1)S(1)}, bf16[128,512]{1,0:T(8,128)(2,1)}, u32[]{:S(2)}) copy-start(bf16[128,512]{1,0:T(8,128)(2,1)} %tokens.1) | copy-start | bytes 393220
  2.5 1.2 %copy-start = (bf16[1,128,4096]{2,1,0:T(8,128)(2,1)S(1)}, bf16[1,128,4096]{2,1,0:T(8,128)(2,1)}, u32[]{:S(2)}) copy-start(bf16[1,128,4096]{2,1,0:T(8,128)(2,1)} %param.9) | copy-start | bytes 3145732

commit v3 on v2

v3 whole, which is shorter than its diff:
```python
import jax
import jax.numpy as jnp
from jax import lax
from jax.experimental import pallas as pl
from jax.experimental.pallas import tpu as pltpu
from jax.sharding import Mesh
from jax.sharding import PartitionSpec as P

NZ, NA, NY, NB = 8, 2, 4, 2
NT = NY * NB
NP = NA * NT
STEPS = NZ // 2 + 1
GATE_STEP = 2
EPS = 1e-06
MESH = pl.DeviceIdType.MESH
F32 = jnp.float32
BF16 = jnp.bfloat16
OFFSETS = [(da, dy, db) for da in range(NA) for dy in range(NY) for db in range(NB)]
X_OFFSETS = [(1, 0, 0), (0, 0, 1), (1, 0, 1)]
Y_OFFSETS = [(0, dy, 0) for dy in range(1, NY)]
ROW_ROW = (((1,), (1,)), ((), ()))
COL_COL = (((0,), (0,)), ((), ()))


def remote(src, dst, send, recv, **where):
    return pltpu.make_async_remote_copy(
        src_ref=src, dst_ref=dst, send_sem=send, recv_sem=recv, device_id=where, device_id_type=MESH
    )


def wait_bytes(like, sem):
    pltpu.make_async_copy(like, like, sem).wait()


class Ring:
    COUNT = 14
    STEPS = ((0, 1, 2, 3), (4, 5, 6, 7), (8, 9, 10, 11), (12, 13))
    LEAD_STEPS = ((0, 1, 4, 5, 2, 3), (8, 9, 6, 7), (12, 10, 11), (13,))

    def __init__(self, z, piece, bulk, sems, steps=STEPS):
        self.z, self.piece, self.bulk, self.steps = z, piece, bulk, steps
        self.right_send, self.right_recv, self.left_send, self.left_recv = sems

    def _copy(self, origin, q, to_right, r):
        piece = self.piece(lax.rem(origin, NZ), q)
        if to_right:
            return remote(piece, piece, self.right_send, self.right_recv.at[r], z=lax.rem(self.z + 1, NZ))
        return remote(piece, piece, self.left_send, self.left_recv.at[r], z=lax.rem(self.z + NZ - 1, NZ))

    def _q(self, r, to_right):
        if r < 12:
            return r % 4
        return 2 * (r - 12) + (0 if to_right else 1)

    def right(self, r):
        return self._copy(self.z + NZ - r // 4, self._q(r, True), True, r)

    def left(self, r):
        return self._copy(self.z + r // 4, self._q(r, False), False, r)

    def start(self, r):
        self.right(r).start()
        self.left(r).start()

    def arrive(self, r):
        self._copy(self.z + 2 * NZ - 1 - r // 4, self._q(r, True), True, r).wait_recv()
        if r < 8:
            self.right(r + 4).start()
        elif r in (8, 10):
            self.right(12 + (r - 8) // 2).start()
        self._copy(self.z + 1 + r // 4, self._q(r, False), False, r).wait_recv()
        if r < 8:
            self.left(r + 4).start()
        elif r in (9, 11):
            self.left(12 + (r - 9) // 2).start()

    def arrive_step(self, k):
        for r in self.steps[k - 1]:
            self.arrive(r)

    def drain(self):
        wait_bytes(self.bulk, self.right_send)
        wait_bytes(self.bulk, self.left_send)


class Plane:
    def __init__(self, me, own, slot, bulk, sems):
        self.me, self.own, self.slot, self.bulk = me, own, slot, bulk
        self.send1, self.recv1, self.send2, self.recv2 = sems

    def _at(self, *offsets):
        a, y, b = self.me
        for da, dy, db in offsets:
            a, y, b = lax.rem(a + NA - da, NA), lax.rem(y + NY - dy, NY), lax.rem(b + NB - db, NB)
        return a, y, b

    def _peer(self, offset):
        a, y, b = self.me
        da, dy, db = offset
        return {"a": lax.rem(a + da, NA), "y": lax.rem(y + dy, NY), "b": lax.rem(b + db, NB)}

    def _first(self, half, i, origin):
        offset = (X_OFFSETS, Y_OFFSETS)[half][i]
        n = 3 * half + i
        return remote(self.own(half), self.slot(origin, half), self.send1, self.recv1.at[n], **self._peer(offset))

    def _second(self, half, i, piece, origin):
        offset = (Y_OFFSETS, X_OFFSETS)[half][i]
        return remote(piece, self.slot(origin, half), self.send2, self.recv2, **self._peer(offset))

    def start(self):
        for half in (0, 1):
            for i in range(3):
                self._first(half, i, self.me).start()
        for half in (0, 1):
            for i in range(3):
                self._second(half, i, self.own(half), self.me).start()

    def relay(self):
        for i in range(3):
            for half in (0, 1):
                origin = self._at((X_OFFSETS, Y_OFFSETS)[half][i])
                self._first(half, i, origin).wait_recv()
                piece = self.slot(origin, half)
                for n in range(3):
                    self._second(half, n, piece, origin).start()

    def wait(self):
        wait_bytes(self.bulk(24), self.recv2)

    def drain(self):
        wait_bytes(self.bulk(6), self.send1)
        wait_bytes(self.bulk(24), self.send2)


def kernel(
    tokens, gain, w_up, down, cot, states, grad,
    tok_v, gain_v, w_v, up_t, down_v, cot_v, squares,
    up_all, down_all, x_all, x1_all, h_all, h_own, c_z, c_all, gain_all, part_send, part_recv, sums, final,
    acc_h, acc_g, g_send, g_recv,
    ex_send, ex_recv, own_sem, gain_send, gain_recv, rs_send, rs_recv, ag_send, ag_recv, f_send, f_recv,
    cz_send, cz_recv, back_send, back_recv, g_ssem, g_rsem,
    u0, u1, u2, u3, d0, d1, d2, d3, h0, h1, h2, h3, x0, x1, x2, x3, c0, c1, c2, c3, gate,
):
    s = lax.axis_index("section")
    z = lax.axis_index("z")
    a = lax.axis_index("a")
    y = lax.axis_index("y")
    b = lax.axis_index("b")
    t = y * NB + b
    place = a * NT + t
    me = (a, y, b)
    first = s == 0
    second = s == 1
    half = w_up.shape[1] // 2
    cols = w_up.shape[0]
    rows, slab = tokens.shape
    sub = rows // NT
    other_a = 1 - a

    def peer(o):
        da, dy, db = OFFSETS[o]
        return {"a": lax.rem(a + da, NA), "y": lax.rem(y + dy, NY), "b": lax.rem(b + db, NB)}

    def source(o):
        da, dy, db = OFFSETS[o]
        return lax.rem(a + NA - da, NA), lax.rem(y + NY - dy, NY), lax.rem(b + NB - db, NB)

    my_rows = pl.ds(pl.multiple_of(half * a, half), half)
    their_rows = pl.ds(pl.multiple_of(half * other_a, half), half)
    my_cols = pl.ds(pl.multiple_of(cols * a, cols), cols)
    their_cols = pl.ds(pl.multiple_of(cols * other_a, cols), cols)
    cot_rows = pl.ds(pl.multiple_of(sub * t, sub), sub)

    def cot_cols(index):
        return pl.ds(pl.multiple_of(slab * index, slab), slab)

    def c_slot(index):
        return c_z.at[index // 4, lax.rem(index, 4)]

    load_w = pltpu.make_async_copy(w_up, w_v, own_sem.at[0])
    load_tok = pltpu.make_async_copy(tokens, tok_v, own_sem.at[1])
    own_x = [
        pltpu.make_async_copy(tokens.at[pl.ds(rows // 2 * i, rows // 2), :], x_all.at[a, t, i], own_sem.at[2 + i])
        for i in (0, 1)
    ]
    load_gain = pltpu.make_async_copy(gain, gain_v, own_sem.at[4])
    load_down = pltpu.make_async_copy(down.at[their_rows, :], down_v, own_sem.at[5])
    own_down = pltpu.make_async_copy(down.at[my_rows, :], down_all.at[z, a], own_sem.at[6])
    load_cot = pltpu.make_async_copy(cot.at[cot_rows, :], cot_v, own_sem.at[7])
    own_cot = pltpu.make_async_copy(cot.at[cot_rows, cot_cols(z)], c_slot(z), own_sem.at[8])
    own_c = pltpu.make_async_copy(c_z, c_all.at[place], own_sem.at[9])
    load_w.start()

    @pl.when(first)
    def _():
        load_tok.start()

    barrier = pltpu.get_barrier_semaphore()
    for dz in range(1, NZ):
        pl.semaphore_signal(barrier, inc=1, device_id={"z": lax.rem(z + dz, NZ)}, device_id_type=MESH)
    for offset in X_OFFSETS + Y_OFFSETS:
        pl.semaphore_signal(barrier, inc=1, device_id=peer(OFFSETS.index(offset)), device_id_type=MESH)
    pl.semaphore_signal(barrier, inc=1, device_id={"section": 1 - s}, device_id_type=MESH)

    @pl.when(first)
    def _():
        own_x[0].start()
        own_x[1].start()

    load_gain.start()
    load_down.start()
    own_down.start()
    load_cot.start()
    own_cot.start()
    load_w.wait()
    up_t[...] = w_v[...].T
    up_all[z, a] = up_t[my_rows, :]
    load_gain.wait()
    gain_all[t] = gain_v[...].astype(F32)

    @pl.when(first)
    def _():
        load_tok.wait()

    pl.semaphore_wait(barrier, NZ - 1 + len(X_OFFSETS) + len(Y_OFFSETS) + 1)

    quarter_rows = half // 2

    def ex_up(i):
        rows_there = pl.ds(pl.multiple_of(half * other_a + quarter_rows * i, quarter_rows), quarter_rows)
        landing = up_all.at[z, a, pl.ds(quarter_rows * i, quarter_rows), :]
        return remote(up_t.at[rows_there, :], landing, ex_send.at[i], ex_recv.at[i], a=other_a)

    def from_up(i):
        landing = up_all.at[z, other_a, pl.ds(quarter_rows * i, quarter_rows), :]
        return remote(landing, landing, ex_send.at[i], ex_recv.at[i], a=other_a)

    ex_down = remote(down_v, down_all.at[z, a], ex_send.at[2], ex_recv.at[2], a=other_a)
    from_down = remote(down_v, down_all.at[z, other_a], ex_send.at[2], ex_recv.at[2], a=other_a)


    def quarter(buffer):
        def piece(origin, q):
            which = a if q < 2 else other_a
            return buffer.at[origin, which, pl.ds(q % 2 * quarter_rows, quarter_rows), :]

        return piece

    up_ring = Ring(z, quarter(up_all), up_all.at[pl.ds(0, 7), 0], (u0, u1, u2, u3), Ring.LEAD_STEPS)
    down_ring = Ring(z, quarter(down_all), down_all.at[pl.ds(0, 7), 0], (d0, d1, d2, d3))
    h_rows = half // 4
    h_ring = Ring(
        z,
        lambda origin, q: h_all.at[origin, pl.ds(q * h_rows, h_rows), :],
        h_all.at[pl.ds(0, 7), pl.ds(0, 2 * h_rows), :],
        (h0, h1, h2, h3),
    )
    x_plane = Plane(
        me,
        lambda i: tok_v.at[pl.ds(rows // 2 * i, rows // 2), :],
        lambda at, i: x_all.at[at[0], at[1] * NB + at[2], i],
        lambda n: x_all.at[:, pl.ds(0, n // 4)] if n == 24 else x_all.at[0, pl.ds(0, n // 2)],
        (x0, x1, x2, x3),
    )
    c_plane = Plane(
        me,
        lambda i: c_z.at[i],
        lambda at, i: c_all.at[at[0] * NT + at[1] * NB + at[2], i],
        lambda n: c_all.at[pl.ds(0, n // 2)],
        (c0, c1, c2, c3),
    )

    gain_pair = gain_all.at[pl.ds(NB * y, NB)]

    def gain_copy(n):
        if n == 0:
            return remote(gain_all.at[t], gain_all.at[t], gain_send.at[0], gain_recv.at[0], b=1 - b)
        return remote(gain_pair, gain_pair, gain_send.at[n], gain_recv.at[n], y=lax.rem(y + n, NY))

    def gain_relay():
        other = gain_all.at[NB * y + 1 - b]
        remote(other, other, gain_send.at[0], gain_recv.at[0], b=1 - b).wait_recv()
        for n in range(1, NY):
            gain_copy(n).start()

    def gain_wait():
        for n in range(1, NY):
            pair = gain_all.at[pl.ds(NB * lax.rem(y + NY - n, NY), NB)]
            remote(pair, pair, gain_send.at[n], gain_recv.at[n], y=lax.rem(y + n, NY)).wait_recv()

    def cz_copy(dz):
        to = lax.rem(z + dz, NZ)
        return remote(cot_v.at[:, cot_cols(to)], c_slot(z), cz_send, cz_recv, z=to)

    def cz_start():
        load_cot.wait()
        for dz in range(1, NZ):
            cz_copy(dz).start()

    cz_bulk = cot_v.at[:, pl.ds(0, (NZ - 1) * slab)]

    def cz_wait():
        own_cot.wait()
        wait_bytes(cz_bulk, cz_recv)

    def width(k):
        return 2 if 0 < k < NZ // 2 else 1

    def slot_of(k, j):
        return lax.rem(z + (k if j else NZ - k), NZ)

    def view(buffer, k, *index):
        return buffer.at[(k, *index)] if width(k) == 2 else buffer.at[(k, *index, 0)]

    def rs_copy(k, o):
        to = peer(o)
        there = to["a"] * NT + to["y"] * NB + to["b"]
        return remote(view(part_send, k, there), view(part_recv, k, o), rs_send.at[k], rs_recv.at[k], **to)

    def rs_bulk(k):
        return view(part_recv, k, pl.ds(1, NP - 1))

    def rs_start(k):
        for o in range(1, NP):
            rs_copy(k, o).start()

    def rs_sum(k, extra):
        wait_bytes(rs_bulk(k), rs_recv.at[k])
        for j in range(width(k)):
            total = part_send[k, place, j].astype(F32)
            if extra is not None:
                total = total + extra(slot_of(k, j))
            for o in range(1, NP):
                total = total + part_recv[k, o, j].astype(F32)
            sums[k, j] = total.astype(BF16)

    def ag_copy(k, o):
        return remote(view(sums, k), view(x1_all, k, place), ag_send.at[k], ag_recv.at[k], section=1, **peer(o))

    def ag_bulk(k):
        return view(x1_all, k, slice(None))

    def ag_start(k):
        for o in range(NP):
            ag_copy(k, o).start()

    def ag_wait(k):
        wait_bytes(ag_bulk(k), ag_recv.at[k])

    def store_part(k, j, which, product):
        part_send[k, :, j, :, pl.ds(which * cols, cols)] = product.astype(BF16).reshape(NP, sub, cols)

    def down_first(k, j):
        for which in range(NA):
            weights = down_all[slot_of(k, j), which]
            store_part(k, j, which, jnp.dot(h_own[...], weights, preferred_element_type=F32))

    def down_second(k, j):
        for which in range(NA):
            hidden = h_all[slot_of(k, j)]
            store_part(k, j, which, lax.dot_general(hidden, down_all[z, which], COL_COL, preferred_element_type=F32))

    def up_start():
        acc_h[...] = jnp.zeros_like(acc_h)
        squares[...] = jnp.zeros_like(squares)

    def up_step(block, index):
        block = block.reshape(NA * rows, slab).astype(F32)
        scaled = (block * gain_all[index]).astype(BF16)
        for which in range(NA):
            acc_h[...] += lax.dot_general(
                scaled[:, which * cols : (which + 1) * cols], up_all[index, which], ROW_ROW, preferred_element_type=F32
            )
        squares[...] += jnp.sum(block * block, axis=1, keepdims=True)

    def finish_hidden():
        inverse_rms = lax.rsqrt(squares[...] * (1.0 / (NT * slab)) + EPS)
        hidden = jax.nn.gelu(acc_h[...] * inverse_rms, approximate=True).astype(BF16)
        h_own[...] = hidden
        h_all[z] = hidden.T

    ahead = lax.rem(t - z + NZ, NZ)
    own_k = jnp.minimum(ahead, NZ - ahead)
    own_j = 1 - jnp.minimum(lax.rem(ahead + NZ - 1, NZ) // 3, 1)
    own_states = x1_all.at[own_k, pl.ds(pl.multiple_of(NT * a, NT), NT), own_j]
    back = remote(own_states, final, back_send, back_recv, section=1 - s)

    def final_copy(k, j):
        return remote(
            sums.at[k, j], final.at[t], f_send.at[min(k, 1)], f_recv, z=slot_of(k, j), y=z // NB, b=lax.rem(z, NB)
        )

    final_local = pltpu.make_async_copy(sums.at[0, 0], final.at[t], f_recv)

    def gradient():
        acc_g[...] = jnp.zeros_like(acc_g)

        @pl.loop(0, NZ)
        def _(index):
            block = c_all[:, index // 4, lax.rem(index, 4)].reshape(NP * sub, slab)
            acc_g[...] += jnp.dot(h_all[index], block, preferred_element_type=F32)

        g_send[...] = acc_g[...].astype(BF16)

    swap = remote(g_send.at[:, their_cols], g_recv, g_ssem, g_rsem, a=other_a)

    @pl.when(first)
    def _():
        ex_up(0).start()
        ex_up(1).start()
        up_ring.start(0)
        up_ring.start(1)
        gain_copy(0).start()
        x_plane.start()
        cz_start()
        up_ring.arrive(0)
        up_ring.arrive(1)
        from_up(0).wait_recv()
        up_ring.start(2)
        from_up(1).wait_recv()
        up_ring.start(3)
        load_down.wait()
        ex_down.start()
        gain_relay()
        x_plane.relay()
        pl.semaphore_signal(gate.at[0], inc=1, device_id={"section": 1 - s}, device_id_type=MESH)
        up_ring.arrive(4)
        up_ring.arrive(5)
        cz_wait()
        own_c.start()
        c_plane.start()
        up_ring.arrive(2)
        up_ring.arrive(3)
        up_start()
        up_ring.arrive_step(2)
        own_x[0].wait()
        own_x[1].wait()
        gain_wait()
        up_ring.arrive_step(3)
        own_down.wait()
        from_down.wait_recv()
        for r in range(4):
            down_ring.start(r)
        x_plane.wait()

        def up_slots(k):
            for j in range(width(k)):
                up_step(x_all[:, slot_of(k, j)], slot_of(k, j))

        up_slots(0)
        up_slots(1)
        up_slots(2)
        up_slots(3)
        up_ring.arrive_step(4)
        up_slots(4)
        finish_hidden()

        def residual(index):
            return x_all[a, index, t // 4, pl.ds(pl.multiple_of(lax.rem(t, 4) * sub, sub), sub), :].astype(F32)

        for k in range(STEPS):
            if k:
                down_ring.arrive_step(k)
            if k == GATE_STEP:
                pl.semaphore_signal(gate.at[1], inc=1, device_id={"section": 1 - s}, device_id_type=MESH)
            for j in range(width(k)):
                down_first(k, j)
            rs_start(k)
            if k == 0:
                c_plane.relay()
            if k >= 2:
                rs_sum(k - 2, residual)
                ag_start(k - 2)
        for r in range(4):
            h_ring.start(r)
        rs_sum(STEPS - 2, residual)
        ag_start(STEPS - 2)
        h_ring.arrive_step(1)
        rs_sum(STEPS - 1, residual)
        ag_start(STEPS - 1)
        for k in range(2, STEPS):
            h_ring.arrive_step(k)
        own_c.wait()
        c_plane.wait()
        gradient()
        swap.start()
        back.wait_recv()
        states[...] = final[...].reshape(rows, slab)

    @pl.when(second)
    def _():
        gain_copy(0).start()
        load_down.wait()
        up_start()
        gain_relay()
        pl.semaphore_wait(gate.at[0], 1)
        ex_up(0).start()
        ex_up(1).start()
        ex_down.start()
        cz_start()
        cz_wait()
        own_c.start()
        c_plane.start()
        c_plane.relay()
        own_down.wait()
        from_up(0).wait_recv()
        from_up(1).wait_recv()
        from_down.wait_recv()
        gain_wait()
        pl.semaphore_wait(gate.at[1], 1)
        for r in range(4):
            up_ring.start(r)

        def up_slots(k):
            ag_wait(k)
            for j in range(width(k)):
                up_step(x1_all[k, :, j], slot_of(k, j))

        up_ring.arrive_step(1)
        up_ring.arrive_step(2)
        up_slots(0)
        up_ring.arrive_step(3)
        up_slots(1)
        up_ring.arrive_step(4)
        up_slots(2)
        up_slots(3)
        up_slots(4)
        finish_hidden()
        for r in range(4):
            h_ring.start(r)
        back.start()
        for k in range(STEPS):
            if k:
                h_ring.arrive_step(k)
            for j in range(width(k)):
                down_second(k, j)
            rs_start(k)

        own_c.wait()
        c_plane.wait()
        gradient()
        swap.start()
        at_home = (z == t)
        for k in range(STEPS):
            rs_sum(k, None)
            for j in range(width(k)):
                if k:
                    final_copy(k, j).start()
                else:
                    @pl.when(at_home)
                    def _():
                        final_local.start()

                    @pl.when(jnp.logical_not(at_home))
                    def _():
                        final_copy(0, 0).start()
        wait_bytes(final, f_recv)
        own_rows = x1_all[own_k, pl.ds(pl.multiple_of(NT * a, NT), NT), own_j].astype(F32)
        states[...] = (own_rows + final[...].astype(F32)).astype(BF16).reshape(rows, slab)

    grad[my_rows, :] = g_send[:, my_cols]
    swap.wait_recv()
    grad[their_rows, :] = g_recv[...]

    swap.wait_send()
    ex_up(0).wait_send()
    ex_up(1).wait_send()
    ex_down.wait_send()
    for n in range(NY):
        gain_copy(n).wait_send()
    wait_bytes(cz_bulk, cz_send)
    for k in range(STEPS):
        wait_bytes(rs_bulk(k), rs_send.at[k])
    c_plane.drain()
    up_ring.drain()
    h_ring.drain()

    @pl.when(first)
    def _():
        x_plane.drain()
        down_ring.drain()
        for k in range(STEPS):
            wait_bytes(ag_bulk(k), ag_send.at[k])

    @pl.when(second)
    def _():
        back.wait_send()
        wait_bytes(final.at[pl.ds(0, NZ - 1)], f_send.at[1])

        @pl.when(z != t)
        def _():
            final_copy(0, 0).wait_send()


def body(tokens, gain, w_up, w_down, cotangent):
    rows, slab = tokens.shape
    cols, hidden = w_up.shape[1:]
    half = hidden // 2
    sub = rows // NT
    dma = pltpu.SemaphoreType.DMA
    vmem = pl.BlockSpec(memory_space=pltpu.VMEM)
    states, grad = pl.pallas_call(
        kernel,
        out_shape=(
            jax.ShapeDtypeStruct((rows, slab), BF16),
            jax.ShapeDtypeStruct((hidden, cols), BF16),
        ),
        in_specs=[pl.BlockSpec(memory_space=pltpu.HBM)] * 5,
        out_specs=(vmem, vmem),
        scratch_shapes=[
            pltpu.VMEM((rows, slab), BF16),
            pltpu.VMEM((1, slab), BF16),
            pltpu.VMEM((cols, hidden), BF16),
            pltpu.VMEM((hidden, cols), BF16),
            pltpu.VMEM((half, cols), BF16),
            pltpu.VMEM((sub, NT * slab), BF16),
            pltpu.VMEM((NA * rows, 1), F32),
            pltpu.VMEM((NZ, NA, half, cols), BF16),
            pltpu.VMEM((NZ, NA, half, cols), BF16),
            pltpu.VMEM((NA, NT, 2, rows // 2, slab), BF16),
            pltpu.VMEM((STEPS, NP, 2, sub, slab), BF16),
            pltpu.VMEM((NZ, half, NA * rows), BF16),
            pltpu.VMEM((NA * rows, half), BF16),
            pltpu.VMEM((2, NZ // 2, sub, slab), BF16),
            pltpu.VMEM((NP, 2, NZ // 2, sub, slab), BF16),
            pltpu.VMEM((NT, 1, slab), F32),
            pltpu.VMEM((STEPS, NP, 2, sub, slab), BF16),
            pltpu.VMEM((STEPS, NP, 2, sub, slab), BF16),
            pltpu.VMEM((STEPS, 2, sub, slab), BF16),
            pltpu.VMEM((NT, sub, slab), BF16),
            pltpu.VMEM((NA * rows, half), F32),
            pltpu.VMEM((half, NA * cols), F32),
            pltpu.VMEM((half, NA * cols), BF16),
            pltpu.VMEM((half, cols), BF16),
            dma((3,)), dma((3,)), dma((10,)), dma((NY,)), dma((NY,)),
            dma((STEPS,)), dma((STEPS,)), dma((STEPS,)), dma((STEPS,)),
            dma((2,)), dma, dma, dma, dma, dma, dma, dma,
        ]
        + [dma, dma((Ring.COUNT,)), dma, dma((Ring.COUNT,))] * 3
        + [dma, dma((6,)), dma, dma] * 2
        + [pltpu.SemaphoreType.REGULAR((2,))],
        compiler_params=pltpu.CompilerParams(
            collective_id=0, has_side_effects=True, vmem_limit_bytes=66 * 1000 * 1000
        ),
    )(tokens, gain, w_up[0], w_down[0], cotangent[0])
    return states[None], grad[None]


def solution(mesh):
    torus = Mesh(
        mesh.devices.reshape(mesh.shape["section"], NZ, NA, NY, NB), ("section", "z", "a", "y", "b")
    )
    dp, tensor = ("z", "a"), ("y", "b")
    in_specs = (
        P(dp, tensor),
        P("section", tensor),
        P("section", dp, tensor),
        P("section", tensor, dp),
        P("section", dp, None),
    )
    out_specs = (P("section", dp, tensor), P("section", tensor, dp))
    return jax.shard_map(body, mesh=torus, in_specs=in_specs, out_specs=out_specs, check_vma=False)
```

time: 111 us -> 97.3 us (0.88)
  Pallas kernels: 106 us -> 93.2 us
  local copies, waits for them, and re-layouts: 4.48 us -> 3.29 us
    pallas_call x1, Pallas kernels: 106 us -> 93.2 us  [body(): pl.pallas_call(kernel, out_shape=(jax.ShapeDtypeStruct((rows, slab), BF16...]
    unnamed x11 -> x2, local copies, waits for them, and re-layouts: 4.48 us -> 3.29 us
where the time goes in v3:
time: 97.3 us; the launch traced here: 97.2 us
  Pallas kernels  93.2 us (96%)
  local copies, waits for them, and re-layouts  3.29 us (3%)
    pallas_call x1, Pallas kernels, body(): pl.pallas_call(kernel, out_shape=(jax.ShapeDtypeStruct((rows, slab), BF16...  93.2 us
    unnamed x2, local copies, waits for them, and re-layouts  3.29 us

profile of v3, /device:TPU:17, one launch (start us, length us, event | category | flops | bytes accessed | tf_op | source)
XLA Modules:
  0.0 97.2 jit_solution(5969521361406668837)
XLA Ops:
  0.6 93.2 %shard_map.68 = (bf16[128,512]{1,0:T(8,128)(2,1)}, bf16[640,256]{1,0:T(8,128)(2,1)}) custom-call(bf16[128,512]{1,0:T(8,128)(2,1)} %tokens.1, bf16[1,512]{1,0:T(2,128)(2,1)} %gain.1, bf16[256,640]{1,0:T(8,128)(2,1)} %bitcast.7, bf16[640,256]{1,0:T(8,128)(2,1)} %bitcast.8, bf16[128,4096]{1,0:T(8,128)(2,1)} %bitcast.5), custom_call_target="tpu_custom_call" | custom-call | tf_op jit(solution)/shard_map/pallas_call | solution.py:603
  93.9 1.6 %copy.9 = bf16[1,128,512]{2,1,0:T(8,128)(2,1)} copy(bf16[1,128,512]{2,1,0:T(8,128)(2,1)} %bitcast.9) | data formatting | bytes 262144
  95.4 1.7 %copy.10 = bf16[1,640,256]{2,1,0:T(8,128)(2,1)} copy(bf16[1,640,256]{2,1,0:T(8,128)(2,1)} %bitcast.6) | data formatting | bytes 655360

commit v4 on v3

--- a/solution.py
+++ b/solution.py
@@ -136,11 +136,11 @@
 def kernel(
     tokens, gain, w_up, down, cot, states, grad,
     tok_v, gain_v, w_v, up_t, down_v, cot_v, squares,
-    up_all, down_all, x_all, x1_all, h_all, h_own, c_z, c_all, gain_all, part_send, part_recv, sums, final,
+    up_all, up_b, down_own, x_all, x1_all, h_all, c_z, c_all, gain_all, part_send, part_recv, sums, z_in, whole, final,
     acc_h, acc_g, g_send, g_recv,
-    ex_send, ex_recv, own_sem, gain_send, gain_recv, rs_send, rs_recv, ag_send, ag_recv, f_send, f_recv,
+    ex_send, ex_recv, bx_send, bx_recv, b_send, b_recv, z_send, z_recv, own_sem, gain_send, gain_recv, rs_send, rs_recv, ag_send, ag_recv, f_send, f_recv,
     cz_send, cz_recv, back_send, back_recv, g_ssem, g_rsem,
-    u0, u1, u2, u3, d0, d1, d2, d3, h0, h1, h2, h3, x0, x1, x2, x3, c0, c1, c2, c3, gate,
+    u0, u1, u2, u3, a0, a1, a2, a3, h0, h1, h2, h3, x0, x1, x2, x3, c0, c1, c2, c3, gate,
 ):
     s = lax.axis_index("section")
     z = lax.axis_index("z")
@@ -186,7 +186,7 @@
     ]
     load_gain = pltpu.make_async_copy(gain, gain_v, own_sem.at[4])
     load_down = pltpu.make_async_copy(down.at[their_rows, :], down_v, own_sem.at[5])
-    own_down = pltpu.make_async_copy(down.at[my_rows, :], down_all.at[z, a], own_sem.at[6])
+    own_down = pltpu.make_async_copy(down.at[my_rows, :], down_own.at[a], own_sem.at[6])
     load_cot = pltpu.make_async_copy(cot.at[cot_rows, :], cot_v, own_sem.at[7])
     own_cot = pltpu.make_async_copy(cot.at[cot_rows, cot_cols(z)], c_slot(z), own_sem.at[8])
     own_c = pltpu.make_async_copy(c_z, c_all.at[place], own_sem.at[9])
@@ -202,6 +202,10 @@
     for offset in X_OFFSETS + Y_OFFSETS:
         pl.semaphore_signal(barrier, inc=1, device_id=peer(OFFSETS.index(offset)), device_id_type=MESH)
     pl.semaphore_signal(barrier, inc=1, device_id={"section": 1 - s}, device_id_type=MESH)
+
+    @pl.when(second)
+    def _():
+        pl.semaphore_signal(barrier, inc=1, device_id={"section": 0, "a": other_a}, device_id_type=MESH)
 
     @pl.when(first)
     def _():
@@ -223,7 +227,15 @@
     def _():
         load_tok.wait()
 
-    pl.semaphore_wait(barrier, NZ - 1 + len(X_OFFSETS) + len(Y_OFFSETS) + 1)
+    greeted = NZ - 1 + len(X_OFFSETS) + len(Y_OFFSETS) + 1
+
+    @pl.when(first)
+    def _():
+        pl.semaphore_wait(barrier, greeted + 1)
+
+    @pl.when(second)
+    def _():
+        pl.semaphore_wait(barrier, greeted)
 
     quarter_rows = half // 2
 
@@ -236,8 +248,30 @@
         landing = up_all.at[z, other_a, pl.ds(quarter_rows * i, quarter_rows), :]
         return remote(landing, landing, ex_send.at[i], ex_recv.at[i], a=other_a)
 
-    ex_down = remote(down_v, down_all.at[z, a], ex_send.at[2], ex_recv.at[2], a=other_a)
-    from_down = remote(down_v, down_all.at[z, other_a], ex_send.at[2], ex_recv.at[2], a=other_a)
+    ex_down = remote(down_v, down_own.at[a], ex_send.at[2], ex_recv.at[2], a=other_a)
+    from_down = remote(down_v, down_own.at[other_a], ex_send.at[2], ex_recv.at[2], a=other_a)
+
+    b_rows = half // 4
+
+    def bx_copy(q):
+        rows_there = pl.ds(pl.multiple_of(half * other_a + b_rows * q, b_rows), b_rows)
+        landing = up_b.at[z, pl.ds(b_rows * q, b_rows), :]
+        return remote(up_t.at[rows_there, :], landing, bx_send, bx_recv.at[q], a=other_a, section=1)
+
+    def bx_wait(q):
+        landing = up_b.at[z, pl.ds(b_rows * q, b_rows), :]
+        pltpu.make_async_copy(landing, landing, bx_recv.at[q]).wait()
+
+    def b_copy(k, j):
+        slot = lax.rem(z + (k if j else NZ - k), NZ)
+        return remote(up_b.at[slot], up_all.at[slot, other_a], b_send, b_recv.at[k], section=0)
+
+    def b_start(k):
+        for j in range(2 if 0 < k < NZ // 2 else 1):
+            b_copy(k, j).start()
+
+    def b_wait(k):
+        wait_bytes(up_b.at[pl.ds(0, 2 if 0 < k < NZ // 2 else 1)], b_recv.at[k])
 
 
     def quarter(buffer):
@@ -248,7 +282,18 @@
         return piece
 
     up_ring = Ring(z, quarter(up_all), up_all.at[pl.ds(0, 7), 0], (u0, u1, u2, u3), Ring.LEAD_STEPS)
-    down_ring = Ring(z, quarter(down_all), down_all.at[pl.ds(0, 7), 0], (d0, d1, d2, d3))
+    own_ring = Ring(
+        z,
+        lambda origin, q: up_all.at[origin, a, pl.ds(q * b_rows, b_rows), :],
+        up_b.at[pl.ds(0, 7), pl.ds(0, 2 * b_rows), :],
+        (a0, a1, a2, a3),
+    )
+    b_ring = Ring(
+        z,
+        lambda origin, q: up_b.at[origin, pl.ds(q * b_rows, b_rows), :],
+        up_b.at[pl.ds(0, 7), pl.ds(0, 2 * b_rows), :],
+        (a0, a1, a2, a3),
+    )
     h_rows = half // 4
     h_ring = Ring(
         z,
@@ -325,18 +370,34 @@
         for o in range(1, NP):
             rs_copy(k, o).start()
 
-    def rs_sum(k, extra):
+    def rs_sum(k):
         wait_bytes(rs_bulk(k), rs_recv.at[k])
         for j in range(width(k)):
             total = part_send[k, place, j].astype(F32)
-            if extra is not None:
-                total = total + extra(slot_of(k, j))
             for o in range(1, NP):
                 total = total + part_recv[k, o, j].astype(F32)
             sums[k, j] = total.astype(BF16)
 
+    def z_copy(k, j):
+        return remote(sums.at[k, j], z_in.at[k, width(k) - 1 - j], z_send, z_recv.at[k], z=slot_of(k, j))
+
+    def z_start(k):
+        for j in range(width(k)):
+            if k:
+                z_copy(k, j).start()
+
+    def z_finish(k):
+        if k:
+            wait_bytes(view(z_in, k), z_recv.at[k])
+        for j in range(width(k)):
+            index = slot_of(k, j)
+            before = x_all[a, index, t // 4, pl.ds(pl.multiple_of(lax.rem(t, 4) * sub, sub), sub), :]
+            added = z_in[k, j] if k else sums[k, j]
+            whole[k, j] = (before.astype(F32) + added.astype(F32)).astype(BF16)
+        ag_start(k)
+
     def ag_copy(k, o):
-        return remote(view(sums, k), view(x1_all, k, place), ag_send.at[k], ag_recv.at[k], section=1, **peer(o))
+        return remote(view(whole, k), view(x1_all, k, place), ag_send.at[k], ag_recv.at[k], section=1, **peer(o))
 
     def ag_bulk(k):
         return view(x1_all, k, slice(None))
@@ -351,15 +412,10 @@
     def store_part(k, j, which, product):
         part_send[k, :, j, :, pl.ds(which * cols, cols)] = product.astype(BF16).reshape(NP, sub, cols)
 
-    def down_first(k, j):
-        for which in range(NA):
-            weights = down_all[slot_of(k, j), which]
-            store_part(k, j, which, jnp.dot(h_own[...], weights, preferred_element_type=F32))
-
-    def down_second(k, j):
+    def down_product(k, j):
         for which in range(NA):
             hidden = h_all[slot_of(k, j)]
-            store_part(k, j, which, lax.dot_general(hidden, down_all[z, which], COL_COL, preferred_element_type=F32))
+            store_part(k, j, which, lax.dot_general(hidden, down_own[which], COL_COL, preferred_element_type=F32))
 
     def up_start():
         acc_h[...] = jnp.zeros_like(acc_h)
@@ -377,7 +433,6 @@
     def finish_hidden():
         inverse_rms = lax.rsqrt(squares[...] * (1.0 / (NT * slab)) + EPS)
         hidden = jax.nn.gelu(acc_h[...] * inverse_rms, approximate=True).astype(BF16)
-        h_own[...] = hidden
         h_all[z] = hidden.T
 
     ahead = lax.rem(t - z + NZ, NZ)
@@ -407,80 +462,65 @@
 
     @pl.when(first)
     def _():
-        ex_up(0).start()
-        ex_up(1).start()
-        up_ring.start(0)
-        up_ring.start(1)
+        for q in range(4):
+            bx_copy(q).start()
+        for r in range(4):
+            own_ring.start(r)
         gain_copy(0).start()
         x_plane.start()
         cz_start()
-        up_ring.arrive(0)
-        up_ring.arrive(1)
-        from_up(0).wait_recv()
-        up_ring.start(2)
-        from_up(1).wait_recv()
-        up_ring.start(3)
-        load_down.wait()
-        ex_down.start()
+        own_ring.arrive_step(1)
         gain_relay()
         x_plane.relay()
         pl.semaphore_signal(gate.at[0], inc=1, device_id={"section": 1 - s}, device_id_type=MESH)
-        up_ring.arrive(4)
-        up_ring.arrive(5)
+        load_down.wait()
+        ex_down.start()
         cz_wait()
         own_c.start()
         c_plane.start()
-        up_ring.arrive(2)
-        up_ring.arrive(3)
         up_start()
-        up_ring.arrive_step(2)
+        own_ring.arrive_step(2)
         own_x[0].wait()
         own_x[1].wait()
         gain_wait()
-        up_ring.arrive_step(3)
+        own_ring.arrive_step(3)
+        c_plane.relay()
+        x_plane.wait()
+
+        def up_slots(k):
+            b_wait(k)
+            for j in range(width(k)):
+                up_step(x_all[:, slot_of(k, j)], slot_of(k, j))
+
+        for k in range(STEPS - 1):
+            up_slots(k)
+        own_ring.arrive_step(4)
+        up_slots(STEPS - 1)
+        finish_hidden()
         own_down.wait()
         from_down.wait_recv()
         for r in range(4):
-            down_ring.start(r)
-        x_plane.wait()
-
-        def up_slots(k):
-            for j in range(width(k)):
-                up_step(x_all[:, slot_of(k, j)], slot_of(k, j))
-
-        up_slots(0)
-        up_slots(1)
-        up_slots(2)
-        up_slots(3)
-        up_ring.arrive_step(4)
-        up_slots(4)
-        finish_hidden()
-
-        def residual(index):
-            return x_all[a, index, t // 4, pl.ds(pl.multiple_of(lax.rem(t, 4) * sub, sub), sub), :].astype(F32)
-
+            h_ring.start(r)
         for k in range(STEPS):
             if k:
-                down_ring.arrive_step(k)
+                h_ring.arrive_step(k)
             if k == GATE_STEP:
                 pl.semaphore_signal(gate.at[1], inc=1, device_id={"section": 1 - s}, device_id_type=MESH)
             for j in range(width(k)):
-                down_first(k, j)
+                down_product(k, j)
             rs_start(k)
-            if k == 0:
-                c_plane.relay()
             if k >= 2:
-                rs_sum(k - 2, residual)
-                ag_start(k - 2)
-        for r in range(4):
-            h_ring.start(r)
-        rs_sum(STEPS - 2, residual)
-        ag_start(STEPS - 2)
-        h_ring.arrive_step(1)
-        rs_sum(STEPS - 1, residual)
-        ag_start(STEPS - 1)
-        for k in range(2, STEPS):
-            h_ring.arrive_step(k)
+                rs_sum(k - 2)
+                z_start(k - 2)
+            if k >= 3:
+                z_finish(k - 3)
+        rs_sum(STEPS - 2)
+        z_start(STEPS - 2)
+        z_finish(STEPS - 3)
+        rs_sum(STEPS - 1)
+        z_start(STEPS - 1)
+        z_finish(STEPS - 2)
+        z_finish(STEPS - 1)
         own_c.wait()
         c_plane.wait()
         gradient()
@@ -491,18 +531,28 @@
     @pl.when(second)
     def _():
         gain_copy(0).start()
-        load_down.wait()
-        up_start()
-        gain_relay()
-        pl.semaphore_wait(gate.at[0], 1)
-        ex_up(0).start()
-        ex_up(1).start()
-        ex_down.start()
-        cz_start()
-        cz_wait()
-        own_c.start()
-        c_plane.start()
-        c_plane.relay()
+        for q in range(4):
+            bx_wait(q)
+            b_ring.start(q)
+        b_start(0)
+        for k in range(1, STEPS):
+            b_ring.arrive_step(k)
+            b_start(k)
+            if k == 1:
+                cz_start()
+                up_start()
+            if k == 2:
+                gain_relay()
+                pl.semaphore_wait(gate.at[0], 1)
+                cz_wait()
+                own_c.start()
+                c_plane.start()
+                load_down.wait()
+                ex_up(0).start()
+                ex_up(1).start()
+                ex_down.start()
+            if k == 4:
+                c_plane.relay()
         own_down.wait()
         from_up(0).wait_recv()
         from_up(1).wait_recv()
@@ -534,7 +584,7 @@
             if k:
                 h_ring.arrive_step(k)
             for j in range(width(k)):
-                down_second(k, j)
+                down_product(k, j)
             rs_start(k)
 
         own_c.wait()
@@ -543,7 +593,7 @@
         swap.start()
         at_home = (z == t)
         for k in range(STEPS):
-            rs_sum(k, None)
+            rs_sum(k)
             for j in range(width(k)):
                 if k:
                     final_copy(k, j).start()
@@ -564,8 +614,6 @@
     grad[their_rows, :] = g_recv[...]
 
     swap.wait_send()
-    ex_up(0).wait_send()
-    ex_up(1).wait_send()
     ex_down.wait_send()
     for n in range(NY):
         gain_copy(n).wait_send()
@@ -573,19 +621,24 @@
     for k in range(STEPS):
         wait_bytes(rs_bulk(k), rs_send.at[k])
     c_plane.drain()
-    up_ring.drain()
+    own_ring.drain()
     h_ring.drain()
 
     @pl.when(first)
     def _():
         x_plane.drain()
-        down_ring.drain()
+        wait_bytes(up_b.at[0], bx_send)
+        wait_bytes(final.at[pl.ds(0, NZ - 1)], z_send)
         for k in range(STEPS):
             wait_bytes(ag_bulk(k), ag_send.at[k])
 
     @pl.when(second)
     def _():
         back.wait_send()
+        up_ring.drain()
+        ex_up(0).wait_send()
+        ex_up(1).wait_send()
+        wait_bytes(up_b, b_send)
         wait_bytes(final.at[pl.ds(0, NZ - 1)], f_send.at[1])
 
         @pl.when(z != t)
@@ -617,23 +670,25 @@
             pltpu.VMEM((sub, NT * slab), BF16),
             pltpu.VMEM((NA * rows, 1), F32),
             pltpu.VMEM((NZ, NA, half, cols), BF16),
-            pltpu.VMEM((NZ, NA, half, cols), BF16),
+            pltpu.VMEM((NZ, half, cols), BF16),
+            pltpu.VMEM((NA, half, cols), BF16),
             pltpu.VMEM((NA, NT, 2, rows // 2, slab), BF16),
             pltpu.VMEM((STEPS, NP, 2, sub, slab), BF16),
             pltpu.VMEM((NZ, half, NA * rows), BF16),
-            pltpu.VMEM((NA * rows, half), BF16),
             pltpu.VMEM((2, NZ // 2, sub, slab), BF16),
             pltpu.VMEM((NP, 2, NZ // 2, sub, slab), BF16),
             pltpu.VMEM((NT, 1, slab), F32),
             pltpu.VMEM((STEPS, NP, 2, sub, slab), BF16),
             pltpu.VMEM((STEPS, NP, 2, sub, slab), BF16),
             pltpu.VMEM((STEPS, 2, sub, slab), BF16),
+            pltpu.VMEM((STEPS, 2, sub, slab), BF16),
+            pltpu.VMEM((STEPS, 2, sub, slab), BF16),
             pltpu.VMEM((NT, sub, slab), BF16),
             pltpu.VMEM((NA * rows, half), F32),
             pltpu.VMEM((half, NA * cols), F32),
             pltpu.VMEM((half, NA * cols), BF16),
             pltpu.VMEM((half, cols), BF16),
-            dma((3,)), dma((3,)), dma((10,)), dma((NY,)), dma((NY,)),
+            dma((3,)), dma((3,)), dma, dma((4,)), dma, dma((STEPS,)), dma, dma((STEPS,)), dma((10,)), dma((NY,)), dma((NY,)),
             dma((STEPS,)), dma((STEPS,)), dma((STEPS,)), dma((STEPS,)),
             dma((2,)), dma, dma, dma, dma, dma, dma, dma,
         ]
@@ -641,9 +696,9 @@
         + [dma, dma((6,)), dma, dma] * 2
         + [pltpu.SemaphoreType.REGULAR((2,))],
         compiler_params=pltpu.CompilerParams(
-            collective_id=0, has_side_effects=True, vmem_limit_bytes=66 * 1000 * 1000
+            collective_id=0, has_side_effects=True, vmem_limit_bytes=48 * 1024 * 1024
         ),
-    )(tokens, gain, w_up[0], w_down[0], cotangent[0])
+    )(*[pltpu.with_memory_space_constraint(x, pltpu.HBM) for x in (tokens, gain, w_up[0], w_down[0], cotangent[0])])
     return states[None], grad[None]
 
 

time: 97.3 us -> 92.7 us (0.953)
  Pallas kernels: 93.2 us -> 90.5 us
  local copies, waits for them, and re-layouts: 3.29 us -> 1.38 us
    pallas_call x1, Pallas kernels: 93.2 us -> 90.5 us  [body(): pl.pallas_call(kernel, out_shape=(jax.ShapeDtypeStruct((rows, slab), BF16...]
    unnamed x2, local copies, waits for them, and re-layouts: 3.29 us -> 1.38 us
where the time goes in v4:
time: 92.7 us; the launch traced here: 92.6 us
  Pallas kernels  90.5 us (98%)
  local copies, waits for them, and re-layouts  1.38 us (1%)
    pallas_call x1, Pallas kernels, body(): pl.pallas_call(kernel, out_shape=(jax.ShapeDtypeStruct((rows, slab), BF16...  90.5 us

profile of v4, /device:TPU:17, one launch (start us, length us, event | category | flops | bytes accessed | tf_op | source)
XLA Modules:
  0.0 92.6 jit_solution(11983875012202380337)
XLA Ops:
  0.6 90.5 %shard_map.68 = (bf16[128,512]{1,0:T(8,128)(2,1)S(1)}, bf16[640,256]{1,0:T(8,128)(2,1)S(1)}) custom-call(bf16[128,512]{1,0:T(8,128)(2,1)} %tokens.1, bf16[1,512]{1,0:T(2,128)(2,1)} %gain.1, bf16[256,640]{1,0:T(8,128)(2,1)} %bitcast.8, bf16[640,256]{1,0:T(8,128)(2,1)} %bitcast.9, bf16[128,4096]{1,0:T(8,128)(2,1)} %bitcast.7), custom_call_target="tpu_custom_call" | custom-call | tf_op jit(solution)/shard_map/pallas_call | solution.py:656
  91.2 0.7 copy.9
  91.8 0.7 copy.10

commit v5 on v4

--- a/solution.py
+++ b/solution.py
@@ -468,23 +468,17 @@
             own_ring.start(r)
         gain_copy(0).start()
         x_plane.start()
-        cz_start()
         own_ring.arrive_step(1)
         gain_relay()
         x_plane.relay()
-        pl.semaphore_signal(gate.at[0], inc=1, device_id={"section": 1 - s}, device_id_type=MESH)
         load_down.wait()
         ex_down.start()
-        cz_wait()
-        own_c.start()
-        c_plane.start()
         up_start()
         own_ring.arrive_step(2)
         own_x[0].wait()
         own_x[1].wait()
         gain_wait()
         own_ring.arrive_step(3)
-        c_plane.relay()
         x_plane.wait()
 
         def up_slots(k):
@@ -514,6 +508,7 @@
                 z_start(k - 2)
             if k >= 3:
                 z_finish(k - 3)
+        cz_start()
         rs_sum(STEPS - 2)
         z_start(STEPS - 2)
         z_finish(STEPS - 3)
@@ -521,6 +516,10 @@
         z_start(STEPS - 1)
         z_finish(STEPS - 2)
         z_finish(STEPS - 1)
+        cz_wait()
+        own_c.start()
+        c_plane.start()
+        c_plane.relay()
         own_c.wait()
         c_plane.wait()
         gradient()
@@ -531,6 +530,7 @@
     @pl.when(second)
     def _():
         gain_copy(0).start()
+        cz_start()
         for q in range(4):
             bx_wait(q)
             b_ring.start(q)
@@ -539,19 +539,17 @@
             b_ring.arrive_step(k)
             b_start(k)
             if k == 1:
-                cz_start()
                 up_start()
-            if k == 2:
-                gain_relay()
-                pl.semaphore_wait(gate.at[0], 1)
                 cz_wait()
                 own_c.start()
                 c_plane.start()
+            if k == 2:
+                gain_relay()
                 load_down.wait()
                 ex_up(0).start()
                 ex_up(1).start()
                 ex_down.start()
-            if k == 4:
+            if k == 3:
                 c_plane.relay()
         own_down.wait()
         from_up(0).wait_recv()

time: 92.7 us -> 91.1 us (0.983)
  Pallas kernels: 90.5 us -> 88.9 us
    pallas_call x1, Pallas kernels: 90.5 us -> 88.9 us  [body(): pl.pallas_call(kernel, out_shape=(jax.ShapeDtypeStruct((rows, slab), BF16...]
where the time goes in v5:
time: 91.1 us; the launch traced here: 91 us
  Pallas kernels  88.9 us (98%)
  local copies, waits for them, and re-layouts  1.38 us (2%)
    pallas_call x1, Pallas kernels, body(): pl.pallas_call(kernel, out_shape=(jax.ShapeDtypeStruct((rows, slab), BF16...  88.9 us

profile of v5, /device:TPU:17, one launch (start us, length us, event | category | flops | bytes accessed | tf_op | source)
XLA Modules:
  0.0 91.0 jit_solution(6227886464575969373)
XLA Ops:
  0.6 88.9 %shard_map.68 = (bf16[128,512]{1,0:T(8,128)(2,1)S(1)}, bf16[640,256]{1,0:T(8,128)(2,1)S(1)}) custom-call(bf16[128,512]{1,0:T(8,128)(2,1)} %tokens.1, bf16[1,512]{1,0:T(2,128)(2,1)} %gain.1, bf16[256,640]{1,0:T(8,128)(2,1)} %bitcast.8, bf16[640,256]{1,0:T(8,128)(2,1)} %bitcast.9, bf16[128,4096]{1,0:T(8,128)(2,1)} %bitcast.7), custom_call_target="tpu_custom_call" | custom-call | tf_op jit(solution)/shard_map/pallas_call | solution.py:654
  89.6 0.7 copy.9
  90.2 0.7 copy.10

commit v6 on v5

--- a/solution.py
+++ b/solution.py
@@ -11,6 +11,7 @@
 NP = NA * NT
 STEPS = NZ // 2 + 1
 GATE_STEP = 2
+PAIRED = ((), (2, 3))
 EPS = 1e-06
 MESH = pl.DeviceIdType.MESH
 F32 = jnp.float32
@@ -136,9 +137,9 @@
 def kernel(
     tokens, gain, w_up, down, cot, states, grad,
     tok_v, gain_v, w_v, up_t, down_v, cot_v, squares,
-    up_all, up_b, down_own, x_all, x1_all, h_all, c_z, c_all, gain_all, part_send, part_recv, sums, z_in, whole, final,
+    up_all, up_b, down_own, x_all, x1_all, h_all, c_z, c_all, gain_all, part_send, part_recv, row_in, col_in, row_out, col_out, row_last, col_last, sums, z_in, whole, final,
     acc_h, acc_g, g_send, g_recv,
-    ex_send, ex_recv, bx_send, bx_recv, b_send, b_recv, z_send, z_recv, own_sem, gain_send, gain_recv, rs_send, rs_recv, ag_send, ag_recv, f_send, f_recv,
+    ex_send, ex_recv, bx_send, bx_recv, b_send, b_recv, z_send, z_recv, own_sem, gain_send, gain_recv, rs_send, rs_recv, mid_send, mid_recv, last_send, last_recv, ag_send, ag_recv, f_send, f_recv,
     cz_send, cz_recv, back_send, back_recv, g_ssem, g_rsem,
     u0, u1, u2, u3, a0, a1, a2, a3, h0, h1, h2, h3, x0, x1, x2, x3, c0, c1, c2, c3, gate,
 ):
@@ -360,23 +361,86 @@
 
     def rs_copy(k, o):
         to = peer(o)
-        there = to["a"] * NT + to["y"] * NB + to["b"]
-        return remote(view(part_send, k, there), view(part_recv, k, o), rs_send.at[k], rs_recv.at[k], **to)
+        piece = part_send.at[k, to["a"], to["y"], to["b"]]
+        landing = view(part_recv, k, o)
+        return remote(piece if width(k) == 2 else piece.at[0], landing, rs_send.at[k], rs_recv.at[k], **to)
 
     def rs_bulk(k):
         return view(part_recv, k, pl.ds(1, NP - 1))
 
-    def rs_start(k):
-        for o in range(1, NP):
-            rs_copy(k, o).start()
-
-    def rs_sum(k):
+    def mid_copies(k):
+        copies = []
+        for i, offset in enumerate(X_OFFSETS):
+            to = peer(OFFSETS.index(offset))
+            piece = part_send.at[k, to["a"], :, to["b"], 0]
+            copies.append(remote(piece, row_in.at[k, i], mid_send.at[2 * k], mid_recv.at[2 * k], **to))
+        for i, offset in enumerate(Y_OFFSETS):
+            to = peer(OFFSETS.index(offset))
+            for n in range(NA):
+                piece = part_send.at[k, n, to["y"], :, 1]
+                landing = col_in.at[k, i, n]
+                copies.append(remote(piece, landing, mid_send.at[2 * k + 1], mid_recv.at[2 * k + 1], **to))
+        return copies
+
+    def last_copies(k):
+        copies = []
+        for i, offset in enumerate(Y_OFFSETS):
+            to = peer(OFFSETS.index(offset))
+            piece = row_out.at[k, to["y"]]
+            copies.append(remote(piece, row_last.at[k, i], last_send.at[2 * k], last_recv.at[2 * k], **to))
+        for i, offset in enumerate(X_OFFSETS):
+            to = peer(OFFSETS.index(offset))
+            piece = col_out.at[k, to["a"], to["b"]]
+            copies.append(remote(piece, col_last.at[k, i], last_send.at[2 * k + 1], last_recv.at[2 * k + 1], **to))
+        return copies
+
+    def rs_start(k, paired=False):
+        copies = mid_copies(k) if paired else [rs_copy(k, o) for o in range(1, NP)]
+        for copy in copies:
+            copy.start()
+
+    def rs_mid(k):
+        wait_bytes(row_in.at[k], mid_recv.at[2 * k])
+        total = part_send[k, a, :, b, 0].astype(F32)
+        for i in range(3):
+            total = total + row_in[k, i].astype(F32)
+        row_out[k] = total.astype(BF16)
+        wait_bytes(col_in.at[k], mid_recv.at[2 * k + 1])
+        total = part_send[k, :, y, :, 1].astype(F32)
+        for i in range(3):
+            total = total + col_in[k, i].astype(F32)
+        col_out[k] = total.astype(BF16)
+        for copy in last_copies(k):
+            copy.start()
+
+    def rs_sum(k, paired=False):
+        if paired:
+            wait_bytes(row_last.at[k], last_recv.at[2 * k])
+            total = row_out[k, y].astype(F32)
+            for i in range(3):
+                total = total + row_last[k, i].astype(F32)
+            sums[k, 0] = total.astype(BF16)
+            wait_bytes(col_last.at[k], last_recv.at[2 * k + 1])
+            total = col_out[k, a, b].astype(F32)
+            for i in range(3):
+                total = total + col_last[k, i].astype(F32)
+            sums[k, 1] = total.astype(BF16)
+            return
         wait_bytes(rs_bulk(k), rs_recv.at[k])
         for j in range(width(k)):
-            total = part_send[k, place, j].astype(F32)
+            total = part_send[k, a, y, b, j].astype(F32)
             for o in range(1, NP):
                 total = total + part_recv[k, o, j].astype(F32)
             sums[k, j] = total.astype(BF16)
+
+    def rs_drain(k, paired=False):
+        if paired:
+            wait_bytes(row_in.at[k], mid_send.at[2 * k])
+            wait_bytes(col_in.at[k], mid_send.at[2 * k + 1])
+            wait_bytes(row_last.at[k], last_send.at[2 * k])
+            wait_bytes(col_last.at[k], last_send.at[2 * k + 1])
+        else:
+            wait_bytes(rs_bulk(k), rs_send.at[k])
 
     def z_copy(k, j):
         return remote(sums.at[k, j], z_in.at[k, width(k) - 1 - j], z_send, z_recv.at[k], z=slot_of(k, j))
@@ -410,7 +474,7 @@
         wait_bytes(ag_bulk(k), ag_recv.at[k])
 
     def store_part(k, j, which, product):
-        part_send[k, :, j, :, pl.ds(which * cols, cols)] = product.astype(BF16).reshape(NP, sub, cols)
+        part_send[k, :, :, :, j, :, pl.ds(which * cols, cols)] = product.astype(BF16).reshape(NA, NY, NB, sub, cols)
 
     def down_product(k, j):
         for which in range(NA):
@@ -502,14 +566,18 @@
                 pl.semaphore_signal(gate.at[1], inc=1, device_id={"section": 1 - s}, device_id_type=MESH)
             for j in range(width(k)):
                 down_product(k, j)
-            rs_start(k)
+            rs_start(k, k in PAIRED[0])
+            if k - 1 in PAIRED[0]:
+                rs_mid(k - 1)
             if k >= 2:
-                rs_sum(k - 2)
+                rs_sum(k - 2, k - 2 in PAIRED[0])
                 z_start(k - 2)
             if k >= 3:
                 z_finish(k - 3)
         cz_start()
-        rs_sum(STEPS - 2)
+        if STEPS - 2 in PAIRED[0]:
+            rs_mid(STEPS - 2)
+        rs_sum(STEPS - 2, STEPS - 2 in PAIRED[0])
         z_start(STEPS - 2)
         z_finish(STEPS - 3)
         rs_sum(STEPS - 1)
@@ -575,6 +643,21 @@
         up_slots(3)
         up_slots(4)
         finish_hidden()
+
+        def send_home(k):
+            rs_sum(k, k in PAIRED[1])
+            for j in range(width(k)):
+                if k:
+                    final_copy(k, j).start()
+                else:
+                    @pl.when(z == t)
+                    def _():
+                        final_local.start()
+
+                    @pl.when(z != t)
+                    def _():
+                        final_copy(0, 0).start()
+
         for r in range(4):
             h_ring.start(r)
         back.start()
@@ -583,26 +666,18 @@
                 h_ring.arrive_step(k)
             for j in range(width(k)):
                 down_product(k, j)
-            rs_start(k)
+            rs_start(k, k in PAIRED[1])
+            if k - 1 in PAIRED[1]:
+                rs_mid(k - 1)
+            if k >= 2:
+                send_home(k - 2)
 
         own_c.wait()
         c_plane.wait()
         gradient()
         swap.start()
-        at_home = (z == t)
-        for k in range(STEPS):
-            rs_sum(k)
-            for j in range(width(k)):
-                if k:
-                    final_copy(k, j).start()
-                else:
-                    @pl.when(at_home)
-                    def _():
-                        final_local.start()
-
-                    @pl.when(jnp.logical_not(at_home))
-                    def _():
-                        final_copy(0, 0).start()
+        for k in (STEPS - 2, STEPS - 1):
+            send_home(k)
         wait_bytes(final, f_recv)
         own_rows = x1_all[own_k, pl.ds(pl.multiple_of(NT * a, NT), NT), own_j].astype(F32)
         states[...] = (own_rows + final[...].astype(F32)).astype(BF16).reshape(rows, slab)
@@ -616,8 +691,6 @@
     for n in range(NY):
         gain_copy(n).wait_send()
     wait_bytes(cz_bulk, cz_send)
-    for k in range(STEPS):
-        wait_bytes(rs_bulk(k), rs_send.at[k])
     c_plane.drain()
     own_ring.drain()
     h_ring.drain()
@@ -625,6 +698,8 @@
     @pl.when(first)
     def _():
         x_plane.drain()
+        for k in range(STEPS):
+            rs_drain(k, k in PAIRED[0])
         wait_bytes(up_b.at[0], bx_send)
         wait_bytes(final.at[pl.ds(0, NZ - 1)], z_send)
         for k in range(STEPS):
@@ -633,6 +708,8 @@
     @pl.when(second)
     def _():
         back.wait_send()
+        for k in range(STEPS):
+            rs_drain(k, k in PAIRED[1])
         up_ring.drain()
         ex_up(0).wait_send()
         ex_up(1).wait_send()
@@ -676,8 +753,14 @@
             pltpu.VMEM((2, NZ // 2, sub, slab), BF16),
             pltpu.VMEM((NP, 2, NZ // 2, sub, slab), BF16),
             pltpu.VMEM((NT, 1, slab), F32),
+            pltpu.VMEM((STEPS, NA, NY, NB, 2, sub, slab), BF16),
             pltpu.VMEM((STEPS, NP, 2, sub, slab), BF16),
-            pltpu.VMEM((STEPS, NP, 2, sub, slab), BF16),
+            pltpu.VMEM((STEPS, 3, NY, sub, slab), BF16),
+            pltpu.VMEM((STEPS, 3, NA, NB, sub, slab), BF16),
+            pltpu.VMEM((STEPS, NY, sub, slab), BF16),
+            pltpu.VMEM((STEPS, NA, NB, sub, slab), BF16),
+            pltpu.VMEM((STEPS, 3, sub, slab), BF16),
+            pltpu.VMEM((STEPS, 3, sub, slab), BF16),
             pltpu.VMEM((STEPS, 2, sub, slab), BF16),
             pltpu.VMEM((STEPS, 2, sub, slab), BF16),
             pltpu.VMEM((STEPS, 2, sub, slab), BF16),
@@ -687,7 +770,8 @@
             pltpu.VMEM((half, NA * cols), BF16),
             pltpu.VMEM((half, cols), BF16),
             dma((3,)), dma((3,)), dma, dma((4,)), dma, dma((STEPS,)), dma, dma((STEPS,)), dma((10,)), dma((NY,)), dma((NY,)),
-            dma((STEPS,)), dma((STEPS,)), dma((STEPS,)), dma((STEPS,)),
+            dma((STEPS,)), dma((STEPS,)), dma((2 * STEPS,)), dma((2 * STEPS,)), dma((2 * STEPS,)), dma((2 * STEPS,)),
+            dma((STEPS,)), dma((STEPS,)),
             dma((2,)), dma, dma, dma, dma, dma, dma, dma,
         ]
         + [dma, dma((Ring.COUNT,)), dma, dma((Ring.COUNT,))] * 3

time: 91.1 us -> 90.1 us (0.989)
    pallas_call x1, Pallas kernels: 88.9 us -> 88 us  [body(): pl.pallas_call(kernel, out_shape=(jax.ShapeDtypeStruct((rows, slab), BF16...]
where the time goes in v6:
time: 90.1 us; the launch traced here: 90 us
  Pallas kernels  88 us (98%)
  local copies, waits for them, and re-layouts  1.38 us (2%)
    pallas_call x1, Pallas kernels, body(): pl.pallas_call(kernel, out_shape=(jax.ShapeDtypeStruct((rows, slab), BF16...  88 us

profile of v6, /device:TPU:17, one launch (start us, length us, event | category | flops | bytes accessed | tf_op | source)
XLA Modules:
  0.0 90.0 jit_solution(2697141300822542072)
XLA Ops:
  0.6 88.0 %shard_map.68 = (bf16[128,512]{1,0:T(8,128)(2,1)S(1)}, bf16[640,256]{1,0:T(8,128)(2,1)S(1)}) custom-call(bf16[128,512]{1,0:T(8,128)(2,1)} %tokens.1, bf16[1,512]{1,0:T(2,128)(2,1)} %gain.1, bf16[256,640]{1,0:T(8,128)(2,1)} %bitcast.8, bf16[640,256]{1,0:T(8,128)(2,1)} %bitcast.9, bf16[128,4096]{1,0:T(8,128)(2,1)} %bitcast.7), custom_call_target="tpu_custom_call" | custom-call | tf_op jit(solution)/shard_map/pallas_call | solution.py:731
  88.6 0.7 copy.9
  89.3 0.7 copy.10

commit v7 on v6

--- a/solution.py
+++ b/solution.py
@@ -523,6 +523,11 @@
         g_send[...] = acc_g[...].astype(BF16)
 
     swap = remote(g_send.at[:, their_cols], g_recv, g_ssem, g_rsem, a=other_a)
+
+    def write_gradient():
+        grad[my_rows, :] = g_send[:, my_cols]
+        swap.wait_recv()
+        grad[their_rows, :] = g_recv[...]
 
     @pl.when(first)
     def _():
@@ -594,6 +599,7 @@
         swap.start()
         back.wait_recv()
         states[...] = final[...].reshape(rows, slab)
+        write_gradient()
 
     @pl.when(second)
     def _():
@@ -678,13 +684,10 @@
         swap.start()
         for k in (STEPS - 2, STEPS - 1):
             send_home(k)
+        write_gradient()
         wait_bytes(final, f_recv)
         own_rows = x1_all[own_k, pl.ds(pl.multiple_of(NT * a, NT), NT), own_j].astype(F32)
         states[...] = (own_rows + final[...].astype(F32)).astype(BF16).reshape(rows, slab)
-
-    grad[my_rows, :] = g_send[:, my_cols]
-    swap.wait_recv()
-    grad[their_rows, :] = g_recv[...]
 
     swap.wait_send()
     ex_down.wait_send()

time: 90.1 us -> 90 us (level)
  no operation moved by 1% of the time
where the time goes in v7:
time: 90 us; the launch traced here: 89.9 us
  Pallas kernels  87.9 us (98%)
  local copies, waits for them, and re-layouts  1.38 us (2%)
    pallas_call x1, Pallas kernels, body(): pl.pallas_call(kernel, out_shape=(jax.ShapeDtypeStruct((rows, slab), BF16...  87.9 us

profile of v7, /device:TPU:17, one launch (start us, length us, event | category | flops | bytes accessed | tf_op | source)
XLA Modules:
  0.0 89.9 jit_solution(3432098171744014794)
XLA Ops:
  0.6 87.9 %shard_map.68 = (bf16[128,512]{1,0:T(8,128)(2,1)S(1)}, bf16[640,256]{1,0:T(8,128)(2,1)S(1)}) custom-call(bf16[128,512]{1,0:T(8,128)(2,1)} %tokens.1, bf16[1,512]{1,0:T(2,128)(2,1)} %gain.1, bf16[256,640]{1,0:T(8,128)(2,1)} %bitcast.8, bf16[640,256]{1,0:T(8,128)(2,1)} %bitcast.9, bf16[128,4096]{1,0:T(8,128)(2,1)} %bitcast.7), custom_call_target="tpu_custom_call" | custom-call | tf_op jit(solution)/shard_map/pallas_call | solution.py:734
  88.6 0.7 copy.9
  89.2 0.7 copy.10
